TPU v7x, 32 devices: a whole 2x2x4 slice. The times are simulated.
32 devices in a mesh: dp: 8 (over y, x, core), tensor: 4 (over z).
Axes of the slice: x: 2, y: 2, z: 4, core: 2. Of those that a mesh axis runs over, the one named last changes fastest.
Arguments:
- tokens: float32 [12544, 768], P(('dp', 'tensor')), may hold values from -6 to 6
- live_clips: int32 [8], P('dp'), may hold values from 1 to 2, as said below
- norm_gains: bfloat16 [3, 768], P(None, 'dp'), may hold values from 0.099609375 to 1.8984375
- qkv_time: bfloat16 [3, 768, 768], P(None, 'dp', 'tensor'), may hold values from -0.21875 to 0.21875
- out_time: bfloat16 [768, 768], P('tensor', 'dp'), may hold values from -0.625 to 0.625
- qkv_space: bfloat16 [3, 768, 768], P(None, 'dp', 'tensor'), may hold values from -0.21875 to 0.21875
- out_space: bfloat16 [768, 768], P('tensor', 'dp'), may hold values from -3.5 to 3.5
- up_weight: bfloat16 [768, 3072], P('dp', 'tensor'), may hold values from -0.21875 to 0.21875
- down_weight: bfloat16 [3072, 768], P('tensor', 'dp'), may hold values from -0.109375 to 0.109375
- cotangent: float32 [12544, 768], P(('dp', 'tensor')), may hold values from -6 to 6
Outputs:
- output: float32 [12544, 768], P(('dp', 'tensor'))
- grad_tokens: float32 [12544, 768], P(('dp', 'tensor'))
- grad_gains: float32 [3, 768], P(None, 'dp')
- grad_qkv_time: float32 [3, 768, 768], P(None, 'dp', 'tensor')
- grad_out_time: float32 [768, 768], P('tensor', 'dp')
- grad_qkv_space: float32 [3, 768, 768], P(None, 'dp', 'tensor')
- grad_out_space: float32 [768, 768], P('tensor', 'dp')
- grad_up: float32 [768, 3072], P('dp', 'tensor')
- grad_down: float32 [3072, 768], P('tensor', 'dp')
Inputs may be any that keep to these rules, and one draw needn't show every extreme that they name: `live_clips`: groups 2i and 2i+1 have equal counts; slots below a group's count are live, the others are padding; some pair of groups has all 2 slots live.
All inputs are finite; a program needn't handle non-finite values.
Results may differ from a plain program's by a relative error of at most 0.038.
Values may be sent and summed in bfloat16 or wider, within the bound.
A program may use at most 128 MiB of HBM per device.

v0:
```python
import functools
import math

import jax
import jax.numpy as jnp
from jax import lax
from jax.experimental import pallas as pl
from jax.experimental.pallas import tpu as pltpu
from jax.sharding import Mesh, PartitionSpec as P

HEAD_DIM = 64
PATCHES = 196
HALF = 4
FRAMES = 8
EPSILON = 1e-06
F32 = jnp.float32
BF16 = jnp.bfloat16
ALL = ("y", "x", "c", "s", "h")
DP = ("y", "x", "c")
TENSOR = ("s", "h")
CLIP = ("c", "h")

NN = (((1,), (0,)), ((), ()))
NT = (((1,), (1,)), ((), ()))
TN = (((0,), (0,)), ((), ()))
BLOCK_ROWS = 96


def mm(a, b, dims=NN):
    return lax.dot_general(a, b, dims, preferred_element_type=F32)


def row_ids(shape, dim, start):
    return lax.broadcasted_iota(jnp.int32, shape, dim) + start


def windows(kind, count):
    if kind == "time":
        return [(0, count, None)]
    found = []
    for frame in range(count // PATCHES):
        low = frame * PATCHES // 16 * 16
        high = min(count, -(-(frame + 1) * PATCHES // 16) * 16)
        found.append((low, high - low, frame))
    return found


def key_bias(start, size, group, stride):
    keys = row_ids((size, size), 0, start)
    if group is None:
        together = keys % stride == row_ids((size, size), 1, start) % stride
    else:
        together = (keys >= group * PATCHES) & (keys < (group + 1) * PATCHES)
    return jnp.where(together, 0.0, -1e30)


def row_valid(start, size, group, width):
    rows = row_ids((size, width), 0, start)
    return (rows >= group * PATCHES) & (rows < (group + 1) * PATCHES)


def normalize(rows, scale_row):
    average = jnp.mean(rows, -1, keepdims=True)
    centred = rows - average
    spread = jnp.mean(centred * centred, -1, keepdims=True)
    return centred * lax.rsqrt(spread + EPSILON) * scale_row


def norm_back(rows, scale_row, grad_normed):
    unused, pullback = jax.vjp(normalize, rows, scale_row)
    return pullback(grad_normed)


def row_block(core, part, quad):
    quad_me = lax.axis_index(("y", "x"))
    block = jnp.bitwise_xor(quad_me, quad) * 2 + jnp.bitwise_xor(core, part)
    return pl.multiple_of(block * BLOCK_ROWS, BLOCK_ROWS)


def head_slices(ref, rows, width, head):
    low = head * HEAD_DIM
    return tuple(ref[rows, part * width + low : part * width + low + HEAD_DIM] for part in range(3))


def put_grads(work, outs):
    if len(outs) == 1:
        outs[0][...] = work[...]
        return
    core = lax.axis_index("c")
    for part, out in enumerate(outs):
        for quad in range(out.shape[0]):
            out[quad] = work[pl.ds(row_block(core, part, quad), out.shape[1]), :]


def attend_kernel(kind, stride, normed_ref, weight_ref, heads_ref, mixed_ref, out_ref, sums, total_ref):
    step = pl.program_id(0)
    count, width = mixed_ref.shape
    heads_ref[...] = mm(normed_ref[...], weight_ref[:, : 3 * width]).astype(BF16)
    sums[...] = jnp.zeros_like(sums)
    for start, size, group in windows(kind, count):
        bias = key_bias(start, size, group, stride)
        rows = pl.ds(start, size)
        for head in range(width // HEAD_DIM):
            low = head * HEAD_DIM
            query, key, value = head_slices(heads_ref, rows, width, head)
            scores = mm(key, query * HEAD_DIM**-0.5, NT) + bias
            weights = jnp.exp(scores - jnp.max(scores, 0, keepdims=True))
            total = jnp.sum(weights, 0, keepdims=True)
            blended = (mm(value.T, weights.astype(BF16)) / total).T
            if group is not None:
                blended = jnp.where(row_valid(start, size, group, HEAD_DIM), blended, 0.0)
            sums[rows, low : low + HEAD_DIM] += blended
    mixed_ref[...] = sums[...].astype(BF16)
    share = mm(mixed_ref[...], weight_ref[:, 3 * width :], NT)

    @pl.when(step == 0)
    def _():
        total_ref[...] = share

    @pl.when(step > 0)
    def _():
        total_ref[...] += share

    @pl.when(step == pl.num_programs(0) - 1)
    def _():
        out_ref[...] = total_ref[...].astype(out_ref.dtype)


def attend_back_kernel(
    kind, stride, normed_ref, weight_ref, heads_ref, mixed_ref, grad_ref, *rest
):
    outs, (out_ref, sums, total_ref, grad_mixed, grad_heads, work) = rest[:-6], rest[-6:]
    step = pl.program_id(0)
    count, width = mixed_ref.shape
    scale = HEAD_DIM**-0.5
    grad_mixed[...] = mm(grad_ref[...], weight_ref[:, 3 * width :]).astype(BF16)
    sums[...] = jnp.zeros_like(sums)
    for start, size, group in windows(kind, count):
        bias = key_bias(start, size, group, stride)
        rows = pl.ds(start, size)
        for head in range(width // HEAD_DIM):
            low = head * HEAD_DIM
            query, key, value = head_slices(heads_ref, rows, width, head)
            query = query * scale
            grad = grad_mixed[rows, low : low + HEAD_DIM]
            if group is not None:
                valid = row_valid(start, size, group, HEAD_DIM)
                grad = jnp.where(valid, grad.astype(F32), 0.0).astype(BF16)
            scores = mm(key, query, NT) + bias
            weights = jnp.exp(scores - jnp.max(scores, 0, keepdims=True))
            weights = weights / jnp.sum(weights, 0, keepdims=True)
            grad_weights = mm(value, grad, NT)
            row_terms = jnp.sum(weights * grad_weights, 0, keepdims=True)
            grad_scores = (weights * (grad_weights - row_terms)).astype(BF16)
            sums[rows, low : low + HEAD_DIM] += (mm(key.T, grad_scores) * scale).T
            low += width
            sums[rows, low : low + HEAD_DIM] += mm(grad_scores, query)
            low += width
            sums[rows, low : low + HEAD_DIM] += mm(weights.astype(BF16), grad)
    grad_heads[...] = sums[...].astype(BF16)
    share = mm(grad_heads[...], weight_ref[:, : 3 * width], NT)

    @pl.when(step == 0)
    def _():
        total_ref[...] = share

    @pl.when(step > 0)
    def _():
        total_ref[...] += share

    @pl.when(step == pl.num_programs(0) - 1)
    def _():
        out_ref[...] = total_ref[...].astype(out_ref.dtype)

    work[:, : 3 * width] = mm(normed_ref[...], grad_heads[...], TN).astype(BF16)
    work[:, 3 * width :] = mm(grad_ref[...], mixed_ref[...], TN).astype(BF16)
    put_grads(work, outs)


def up_kernel(normed_ref, weight_ref, hidden_ref, slope_ref):
    pre_act = mm(normed_ref[...], weight_ref[...])
    cdf = 0.5 * (1.0 + lax.erf(pre_act * 0.5**0.5))
    hidden_ref[...] = (pre_act * cdf).astype(BF16)
    density = jnp.exp(-0.5 * pre_act * pre_act) * (0.5 / math.pi) ** 0.5
    slope_ref[...] = (cdf + pre_act * density).astype(slope_ref.dtype)


def down_kernel(hidden_ref, weight_ref, out_ref):
    share = mm(hidden_ref[...], weight_ref[...], NT)

    @pl.when(pl.program_id(0) == 0)
    def _():
        out_ref[...] = share

    @pl.when(pl.program_id(0) > 0)
    def _():
        out_ref[...] += share


def down_back_kernel(grad_ref, weight_ref, hidden_ref, slope_ref, *rest):
    outs, (grad_pre_ref, work) = rest[:-2], rest[-2:]
    grad_hidden = mm(grad_ref[...], weight_ref[...])
    grad_pre_ref[...] = (grad_hidden * slope_ref[...].astype(F32)).astype(BF16)
    work[...] = mm(grad_ref[...], hidden_ref[...], TN).astype(BF16)
    put_grads(work, outs)


def up_back_kernel(normed_ref, weight_ref, grad_pre_ref, *rest):
    outs, (out_ref, work) = rest[:-2], rest[-2:]
    share = mm(grad_pre_ref[...], weight_ref[...], NT)

    @pl.when(pl.program_id(0) == 0)
    def _():
        out_ref[...] = share

    @pl.when(pl.program_id(0) > 0)
    def _():
        out_ref[...] += share

    work[...] = mm(normed_ref[...], grad_pre_ref[...], TN).astype(BF16)
    put_grads(work, outs)


def whole_spec(array):
    return pl.BlockSpec(array.shape, lambda i: (0,) * array.ndim)


def step_spec(array):
    rest = array.shape[1:]
    return pl.BlockSpec((None,) + rest, lambda i: (i,) + (0,) * len(rest))


def phase(kernel, name, inputs, outputs, scratch=(), cost=0):
    blocks = [a for a in inputs if a.ndim > 2][0].shape[0]
    spec = lambda a: whole_spec(a) if a.ndim == 2 else step_spec(a)
    return pl.pallas_call(
        kernel,
        grid=(blocks,),
        in_specs=[spec(a) for a in inputs],
        out_specs=[spec(a) for a in outputs],
        out_shape=outputs,
        scratch_shapes=list(scratch),
        cost_estimate=pl.CostEstimate(
            flops=int(cost * 800e6), bytes_accessed=int(cost * 1e6), transcendentals=0
        ),
        name=name,
    )(*inputs)


def shaped(*shape, dtype=BF16):
    return jax.ShapeDtypeStruct(shape, dtype)


def grad_shapes(weight, routed):
    blocks, depth, lanes = weight.shape
    if not routed:
        return [shaped(blocks, depth, lanes)]
    rows = BLOCK_ROWS
    return [shaped(blocks, depth // rows // 2, rows, lanes) for part in range(2)]


def attend(kind, normed, weight, stride, out_dtype):
    blocks, depth, lanes = weight.shape
    count, width = normed.shape[0], lanes // 4
    return phase(
        functools.partial(attend_kernel, kind, stride),
        kind + "_attend",
        (normed, weight),
        (
            shaped(blocks, count, 3 * width),
            shaped(blocks, count, width),
            shaped(count, depth, dtype=out_dtype),
        ),
        (pltpu.VMEM((count, width), F32), pltpu.VMEM((count, depth), F32)),
        cost=14,
    )


def attend_back(kind, normed, weight, heads, mixed, grad, stride, out_dtype, routed):
    blocks, depth, lanes = weight.shape
    count, width = normed.shape[0], lanes // 4
    *grads, out = phase(
        functools.partial(attend_back_kernel, kind, stride),
        kind + "_attend_back",
        (normed, weight, heads, mixed, grad),
        (*grad_shapes(weight, routed), shaped(count, depth, dtype=out_dtype)),
        (
            pltpu.VMEM((count, 3 * width), F32),
            pltpu.VMEM((count, depth), F32),
            pltpu.VMEM((count, width), BF16),
            pltpu.VMEM((count, 3 * width), BF16),
            pltpu.VMEM((depth, lanes), BF16),
        ),
        cost=20,
    )
    return grads, out


def along(piece, axes, distance):
    size = lax.axis_size(axes)
    return lax.ppermute(piece, axes, [(i, i ^ distance) for i in range(size)])


def after(piece, earlier):
    return piece + earlier[:1, :1] * 0


def gather_plain(shard):
    every = lax.all_gather(shard, TENSOR, axis=0, tiled=False)
    return lax.all_gather(every.reshape(-1, *shard.shape), DP, axis=1, tiled=True)


def reduce_plain(grads):
    part = lax.psum_scatter(grads[0], TENSOR, scatter_dimension=0, tiled=True)[0]
    return lax.psum_scatter(part, DP, scatter_dimension=0, tiled=True).astype(F32)


def by_member(parts, me):
    return jnp.stack(
        [
            lax.dynamic_index_in_dim(parts, jnp.bitwise_xor(me, k), 0, keepdims=False)
            for k in range(parts.shape[0])
        ]
    )


def to_patches(rows, members):
    share, columns = PATCHES // members, rows.shape[1]
    me = lax.axis_index(CLIP)
    parts = rows.reshape(-1, members, share, columns).transpose(1, 0, 2, 3)
    parts = [
        lax.dynamic_index_in_dim(parts, jnp.bitwise_xor(me, k), 0, keepdims=False)
        for k in range(members)
    ]
    parts = [parts[0]] + [along(parts[k], CLIP, k) for k in range(1, members)]
    return by_member(jnp.stack(parts), me).reshape(-1, columns)


def to_frames(rows, members):
    share, columns = PATCHES // members, rows.shape[1]
    me = lax.axis_index(CLIP)
    parts = by_member(rows.reshape(members, -1, share, columns), me)
    parts = [parts[0]] + [along(parts[k], CLIP, k) for k in range(1, members)]
    parts = jnp.stack(parts)
    order = jnp.bitwise_xor(me, jnp.arange(members))
    parts = [
        lax.dynamic_index_in_dim(parts, jnp.bitwise_xor(me, k), 0, keepdims=False)
        for k in range(members)
    ]
    return jnp.stack(parts, 1).reshape(-1, columns)


CHUNKS = 4
STEPS = 4
PAD = 56


def place():
    return {axis: lax.axis_index(axis) for axis in ALL}


def moved(here, **flips):
    return tuple(here[a] + flips.get(a, 0) * (1 - 2 * here[a]) for a in ALL)


def dp_row(here, y=0, x=0, c=0):
    to = lambda a, flip: here[a] + flip * (1 - 2 * here[a])
    return to("y", y) * 4 + to("x", x) * 2 + to("c", c)


def remote(source, target, sent, received, device):
    return pltpu.make_async_remote_copy(
        src_ref=source,
        dst_ref=target,
        send_sem=sent,
        recv_sem=received,
        device_id=device,
        device_id_type=pl.DeviceIdType.MESH,
    )


def peers(here):
    found = [moved(here, s=j // 2, h=j % 2) for j in range(1, 4)]
    found += [moved(here, y=r // 4, x=r // 2 % 2, c=r % 2) for r in range(1, 8)]
    return found + [moved(here, c=1, h=1)]


def greet(here, what):
    barrier = pltpu.get_barrier_semaphore()
    everyone = peers(here)
    if what == "answer":
        pl.semaphore_wait(barrier, len(everyone))
        return
    for device in everyone:
        pl.semaphore_signal(
            barrier, inc=1, device_id=device, device_id_type=pl.DeviceIdType.MESH
        )


class Exchange:
    def __init__(self, here, out, back, sent, received):
        self.here, self.out, self.back = here, out, back
        self.sent, self.received = sent, received
        self.me = here["c"] * 2 + here["h"]

    def device(self, member):
        return tuple({"c": member // 2, "h": member % 2}.get(a, self.here[a]) for a in ALL)

    def start(self, member):
        @pl.when(self.me != member)
        def _():
            remote(
                self.out.at[member],
                self.back.at[self.me],
                self.sent.at[member],
                self.received.at[self.me],
                self.device(member),
            ).start()

        @pl.when(self.me == member)
        def _():
            self.back[member] = self.out[member]

    def finish(self, member):
        @pl.when(self.me != member)
        def _():
            remote(
                self.out.at[member],
                self.back.at[member],
                self.sent.at[member],
                self.received.at[member],
                self.device(member),
            ).wait()

    def send(self, rows_ref, first_row):
        share = PATCHES // 4
        for member in range(4):
            for frame in range(2):
                low = first_row(member, frame)
                self.out[member, frame, :share, :] = rows_ref[low : low + share, :].astype(BF16)
            self.start(member)

    def take(self, rows_ref, first_row):
        share = PATCHES // 4
        for member in range(4):
            self.finish(member)
            for frame in range(2):
                low = first_row(member, frame)
                rows_ref[low : low + share, :] = self.back[member, frame, :share, :].astype(F32)

    @staticmethod
    def by_frame(member, frame):
        return frame * PATCHES + member * (PATCHES // 4)

    @staticmethod
    def by_share(member, frame):
        return (member * 2 + frame) * (PATCHES // 4)

    def send_frames(self, rows_ref):
        self.send(rows_ref, self.by_frame)

    def take_patches(self, rows_ref):
        self.take(rows_ref, self.by_share)

    def send_patches(self, rows_ref):
        self.send(rows_ref, self.by_share)

    def take_frames(self, rows_ref):
        self.take(rows_ref, self.by_frame)


def by_rows(count, body, size=56):
    def step(i, carry):
        body(pl.ds(pl.multiple_of(i * size, size), size))
        return carry

    lax.fori_loop(0, count // size, step, 0)


def row_stats(rows):
    average = jnp.mean(rows, -1, keepdims=True)
    centred = rows - average
    spread = jnp.mean(centred * centred, -1, keepdims=True)
    return centred, lax.rsqrt(spread + EPSILON)


def attend_block(kind, stride, t, normed, weight, heads_ref, mixed_ref, sums, bias_ref):
    count, width = mixed_ref.shape[1:]
    heads_ref[t] = mm(normed, weight[:, : 3 * width]).astype(BF16)
    heads = heads_ref.at[t]
    sums[...] = jnp.zeros_like(sums)
    for start, size, group in windows(kind, count):
        bias = bias_ref[...] if group is None else key_bias(start, size, group, stride)
        rows = pl.ds(start, size)
        for head in range(width // HEAD_DIM):
            low = head * HEAD_DIM
            query, key, value = head_slices(heads, rows, width, head)
            scores = mm(key, query * HEAD_DIM**-0.5, NT) + bias
            weights = jnp.exp(scores - jnp.max(scores, 0, keepdims=True))
            total = jnp.sum(weights, 0, keepdims=True)
            blended = (mm(value.T, weights.astype(BF16)) / total).T
            if group is not None:
                blended = jnp.where(row_valid(start, size, group, HEAD_DIM), blended, 0.0)
            sums[rows, low : low + HEAD_DIM] += blended
    mixed_ref[t] = sums[...].astype(BF16)
    return mm(mixed_ref[t], weight[:, 3 * width :], NT)


def attend_back_block(
    kind, stride, heads, mixed, grad, normed, weight, grad_mixed, sums, grad_heads, bias_ref
):
    count, width = mixed.shape
    scale = HEAD_DIM**-0.5
    grad_mixed[...] = mm(grad[...], weight[:, 3 * width :]).astype(BF16)
    sums[...] = jnp.zeros_like(sums)
    for start, size, group in windows(kind, count):
        bias = bias_ref[...] if group is None else key_bias(start, size, group, stride)
        rows = pl.ds(start, size)
        for head in range(width // HEAD_DIM):
            low = head * HEAD_DIM
            query, key, value = head_slices(heads, rows, width, head)
            query = query * scale
            grad_here = grad_mixed[rows, low : low + HEAD_DIM]
            if group is not None:
                valid = row_valid(start, size, group, HEAD_DIM)
                grad_here = jnp.where(valid, grad_here.astype(F32), 0.0).astype(BF16)
            scores = mm(key, query, NT) + bias
            weights = jnp.exp(scores - jnp.max(scores, 0, keepdims=True))
            weights = weights * (1.0 / jnp.sum(weights, 0, keepdims=True))
            grad_weights = mm(value, grad_here, NT)
            row_terms = jnp.sum(weights * grad_weights, 0, keepdims=True)
            grad_scores = (weights * (grad_weights - row_terms)).astype(BF16)
            sums[rows, low : low + HEAD_DIM] += (mm(key.T, grad_scores) * scale).T
            low += width
            sums[rows, low : low + HEAD_DIM] += mm(grad_scores, query)
            low += width
            sums[rows, low : low + HEAD_DIM] += mm(weights.astype(BF16), grad_here)
    grad_heads[...] = sums[...].astype(BF16)
    return mm(grad_heads[...], weight[:, : 3 * width], NT)


EVENT_NAMES = ("zs", "line", "relay", "across", "core", "first", "second", "third")
BLOCK_ORDER = (1, 2, 3, 0)
ORDER = (
    ("go",),
    ("zs", 0, 1), ("zs", 0, 2), ("zs", 0, 3), ("line", 0, 0), ("line", 1, 0), ("ln0",),
    ("line", 2, 0), ("mask",), ("line", 3, 0), ("line", 0, 1), ("zs", 1, 1), ("line", 0, 2),
    ("zs", 1, 2), ("relay", 0, 0), ("zs", 1, 3), ("line", 0, 3), ("takeE0",), ("relay", 0, 1),
    ("zs", 2, 1), ("relay", 0, 2), ("line", 1, 1), ("zs", 2, 2), ("across", 0, 0),
    ("relay", 1, 0), ("relay", 0, 3), ("across", 0, 2), ("zs", 2, 3), ("line", 1, 2),
    ("across", 0, 1), ("line", 1, 3), ("zs", 3, 1), ("across", 0, 3), ("P0", 0), ("relay", 1, 1),
    ("across", 1, 0), ("zs", 3, 2), ("P0", 1), ("relay", 1, 2), ("line", 2, 1), ("zs", 3, 3),
    ("P0", 2), ("relay", 1, 3), ("relay", 2, 0), ("P0", 3), ("across", 1, 1), ("across", 1, 2),
    ("line", 2, 2), ("exch1",), ("relay", 3, 0), ("line", 2, 3), ("across", 2, 0),
    ("across", 1, 3), ("relay", 2, 1), ("relay", 2, 2), ("line", 3, 1), ("across", 3, 0),
    ("ln1",), ("relay", 2, 3), ("line", 3, 2), ("P1", 0), ("across", 2, 1), ("across", 2, 2),
    ("line", 3, 3), ("P1", 1), ("relay", 3, 1), ("P1", 2), ("across", 2, 3), ("P1", 3),
    ("relay", 3, 2), ("ln2",), ("relay", 3, 3), ("up", 0), ("across", 3, 1), ("up", 1),
    ("across", 3, 2), ("core", 0), ("up", 2), ("across", 3, 3), ("core", 1), ("up", 3),
    ("core", 2), ("dn", 0), ("first", 0), ("core", 3), ("dn", 1), ("first", 1), ("dn", 2),
    ("dn", 3), ("first", 2), ("B1", 0), ("second", 0), ("B1", 1), ("first", 3), ("core", 4),
    ("B1", 2), ("second", 1), ("core", 5), ("second", 2), ("B1", 3), ("second", 3), ("nb2",),
    ("core", 6), ("core", 7), ("B2", 0), ("first", 4), ("first", 5), ("B2", 1), ("third", 0),
    ("first", 6), ("first", 7), ("core", 8), ("B2", 2), ("second", 4), ("second", 5),
    ("second", 6), ("core", 9), ("B2", 3), ("second", 7), ("first", 8), ("core", 10), ("nb1",),
    ("first", 9), ("core", 11), ("second", 8), ("first", 10), ("second", 9), ("third", 1),
    ("first", 11), ("second", 10), ("takeE2",), ("B3", 0), ("second", 11), ("B3", 1),
    ("core", 12), ("B3", 2), ("third", 2), ("core", 13), ("B3", 3), ("first", 12), ("core", 14),
    ("exch3",), ("first", 13), ("core", 15), ("second", 12), ("first", 14), ("nb0",),
    ("second", 13), ("gain",), ("first", 15), ("second", 14), ("second", 15), ("third", 3),
)


def after_each(order):
    found, events = {}, []
    for item in order:
        if item[0] in EVENT_NAMES:
            events.append(item)
        else:
            events = found.setdefault(item, [])
    return found


AFTER = after_each(ORDER)


def layer_kernel(
    live_ref,
    tokens_hbm,
    cotangent_hbm,
    gain_hbm,
    qkv_time_hbm,
    out_time_hbm,
    qkv_space_hbm,
    out_space_hbm,
    up_hbm,
    down_hbm,
    weight_ref,
    out_ref,
    stream_ref,
    own_ref,
    own_gain_ref,
    tokens_ref,
    gain_ref,
    qkv_time_ref,
    out_time_ref,
    qkv_space_ref,
    out_space_ref,
    shard_ref,
    held,
    normed_time_ref,
    time_heads_ref,
    time_mixed_ref,
    after_time_ref,
    normed_space_ref,
    space_heads_ref,
    space_mixed_ref,
    after_space_ref,
    normed_mlp_ref,
    hidden_ref,
    slope_ref,
    low_ref,
    rows_ref,
    total_ref,
    mixed_sums,
    sums,
    grad_mixed,
    grad_heads,
    bias_ref,
    work,
    keep,
    came,
    first,
    second,
    third,
    gains_ref,
    gain_sums,
    gain_line,
    gain_out,
    gain_parts,
    swap_out,
    swap_back,
    piece_sent,
    piece_here,
    core_sent,
    core_here,
    first_sent,
    first_here,
    second_sent,
    second_here,
    third_sent,
    third_here,
    gain_sent,
    gain_here,
    swap_sent,
    swap_here,
    held_sem,
    own_sem,
    load_sem,
    credit,
):
    here = place()
    count, columns = tokens_ref.shape
    width = time_mixed_ref.shape[2]
    own_row = dp_row(here)
    last = CHUNKS * STEPS - 1
    live = jnp.where(here["s"] < live_ref[0], 1.0, 0.0).astype(F32)

    loads = [
        pltpu.make_async_copy(source, target, load_sem.at[i])
        for i, (source, target) in enumerate(
            (
                (gain_hbm, gain_ref),
                (qkv_time_hbm, qkv_time_ref),
                (out_time_hbm, out_time_ref),
                (qkv_space_hbm, qkv_space_ref),
                (out_space_hbm, out_space_ref),
                (up_hbm, shard_ref.at[2]),
                (down_hbm, shard_ref.at[3]),
                (tokens_hbm, tokens_ref),
                (cotangent_hbm, stream_ref),
            )
        )
    ]
    greet(here, "call")
    for load in loads:
        load.start()
    for load in loads[:5]:
        load.wait()

    for k, qkv, out in ((0, qkv_time_ref, out_time_ref), (1, qkv_space_ref, out_space_ref)):
        for c in range(3):
            shard_ref[k, :, c * width : (c + 1) * width] = qkv[c]
        shard_ref[k, :, 3 * width :] = out[...].astype(F32).T.astype(BF16)
    own_gains = gain_ref.shape[1]
    gain_out[0, : gain_ref.shape[0], :own_gains] = gain_ref[...].astype(F32)
    for load in loads[5:7]:
        load.wait()
    greet(here, "answer")

    def row_of(part, r):
        return dp_row(here, y=r // 2, x=r % 2, c=part)

    def slot_of(k, j, row):
        return weight_ref.at[k, j, pl.ds(pl.multiple_of(row * BLOCK_ROWS, BLOCK_ROWS), BLOCK_ROWS)]

    def arrived(k, part, r, j):
        slot = slot_of(k, j, row_of(part, r))
        remote(
            slot, slot, piece_sent.at[k, 0, 0], piece_here.at[k, part, r, j], moved(here, c=1)
        ).wait_recv()

    def send(source, k, j, r, sem, part, r_there, **flips):
        remote(
            source,
            slot_of(k, j, row_of(0, r)),
            piece_sent.at[k, sem, j],
            piece_here.at[k, part, r_there, j],
            moved(here, **flips),
        ).start()

    def piece(k, j, r):
        return slot_of(k, j, row_of(0, r))

    def along_line(k, j):
        remote(
            shard_ref.at[k],
            slot_of(k, j, own_row),
            piece_sent.at[k, 0, j],
            piece_here.at[k, 0, 0, j],
            moved(here, s=j // 2, h=j % 2),
        ).start()

    def spread(source, k, j):
        send(source, k, j, 0, 1, 0, 1, x=1)
        send(source, k, j, 0, 2, 0, 2, y=1)
        send(source, k, j, 0, 4, 1, 0, c=1)

    def line(k, j):
        if j:
            arrived(k, 0, 0, j)
        spread(piece(k, j, 0) if j else shard_ref.at[k], k, j)

    def relay(k, j):
        up = j // 2
        arrived(k, 0, 1, j)
        send(piece(k, j, 1), k, j, 1, 5, 1, 1, c=1)
        arrived(k, 0, 2, j)
        send(piece(k, j, 2), k, j, 2, 6, 1, 2, c=1)
        source = slot_of(k, j, dp_row(here, y=up, x=1 - up))
        remote(
            source,
            source,
            piece_sent.at[k, 3, j],
            piece_here.at[k, 0, 3, j],
            moved(here, y=1 - up, x=up),
        ).start()

    def across(k, j):
        arrived(k, 0, 3, j)
        send(piece(k, j, 3), k, j, 3, 7, 1, 3, c=1)

    def fetch(k, t):
        return pltpu.make_async_copy(weight_ref.at[k, t], held.at[t], held_sem.at[t])

    def ready(k):
        for j in range(STEPS):
            for r in range(4):
                arrived(k, 1, r, j)
        for t in BLOCK_ORDER:
            fetch(k, t).start()

    def weight(k, t):
        fetch(k, t).wait()
        return held.at[t]

    def stored(k):
        return pltpu.make_async_copy(shard_ref.at[k], slot_of(k, 0, own_row), own_sem.at[k])

    half_lanes = keep.shape[4]
    swapped = (0, 2, 1, 3)

    def grad_rows(part, quad):
        row = dp_row(here, y=quad // 2, x=quad % 2, c=part)
        return pl.ds(pl.multiple_of(row * BLOCK_ROWS, BLOCK_ROWS), BLOCK_ROWS)

    def core_copy(step, quad):
        return remote(
            work.at[step % 2, grad_rows(1, quad)],
            came.at[step % 4, quad],
            core_sent.at[step % 2, quad],
            core_here.at[step % 4, quad],
            moved(here, c=1),
        )

    def first_copy(step, half):
        return remote(
            keep.at[step, pl.ds(2, 2), half],
            first.at[step, half],
            first_sent.at[step, half],
            first_here.at[step, half],
            moved(here, y=1 - half, x=half),
        )

    def second_copy(step, half):
        return remote(
            keep.at[step, 1, half],
            second.at[step, half],
            second_sent.at[step, half],
            second_here.at[step, half],
            moved(here, y=half, x=1 - half),
        )

    def third_copy(step):
        j = BLOCK_ORDER[step % STEPS]
        return remote(
            keep.at[step, 0],
            third.at[step],
            third_sent.at[step],
            third_here.at[step],
            moved(here, s=j // 2, h=j % 2),
        )

    def begin(step):
        @pl.when(step >= 2)
        def _():
            for quad in range(4):
                core_copy(step - 2, quad).wait_send()

        return work.at[step % 2]

    def emit(step):
        @pl.when(step >= 4)
        def _():
            pl.semaphore_wait(credit, 1)

        for quad in range(4):
            core_copy(step, quad).start()

    def take_core(step):
        for quad in range(4):
            core_copy(step, quad).wait_recv()
        for index in (2, 3, 1, 0):
            for half in range(2):
                quad = swapped[index] if half else index
                lanes = slice(half * half_lanes, (half + 1) * half_lanes)
                own = work[step % 2, grad_rows(0, quad), lanes].astype(F32)
                both = own + came[step % 4, quad, :, lanes].astype(F32)
                keep[step, index, half] = both.astype(BF16)
                if index == 3:
                    first_copy(step, half).start()
        if step <= last - 4:
            pl.semaphore_signal(
                credit,
                inc=1,
                device_id=moved(here, c=1),
                device_id_type=pl.DeviceIdType.MESH,
            )

    def take_first(step):
        for half in range(2):
            first_copy(step, half).wait_recv()
            for index in (1, 0):
                both = keep[step, index, half].astype(F32) + first[step, half, index].astype(F32)
                keep[step, index, half] = both.astype(BF16)
                if index:
                    second_copy(step, half).start()

    def take_second(step):
        for half in range(2):
            second_copy(step, half).wait_recv()
            both = keep[step, 0, half].astype(F32) + second[step, half].astype(F32)
            keep[step, 0, half] = both.astype(BF16)
        if BLOCK_ORDER[step % STEPS]:
            third_copy(step).start()

    def take_third(index):
        steps = [index * STEPS + i for i in range(STEPS)]
        for step in steps:
            if BLOCK_ORDER[step % STEPS]:
                third_copy(step).wait_recv()
        for half in range(2):
            total = jnp.zeros((BLOCK_ROWS, half_lanes), F32)
            for step in steps:
                source = third[step, half] if BLOCK_ORDER[step % STEPS] else keep[step, 0, half]
                total = total + source.astype(F32)
            own_ref[index, :, half * half_lanes : (half + 1) * half_lanes] = total

    events = {
        "zs": along_line,
        "line": line,
        "relay": relay,
        "across": across,
        "core": take_core,
        "first": take_first,
        "second": take_second,
        "third": take_third,
    }

    def follow(item):
        for name, *args in AFTER.get(item, ()):
            events[name](*args)

    def loop(name, body):
        def step(i, carry):
            body(i, (i + 1) % STEPS)
            for c in range(STEPS - 1):
                if AFTER.get((name, c)):

                    @pl.when(i == c)
                    def _(c=c):
                        follow((name, c))

            return carry

        lax.fori_loop(0, STEPS, step, 0)
        follow((name, STEPS - 1))

    def layer_norm(source_ref, gain, target_ref):
        def body(rows):
            centred, scale = row_stats(source_ref[rows, :])
            target_ref[rows, :] = (centred * scale * gains_ref[gain : gain + 1, :]).astype(
                target_ref.dtype
            )

        by_rows(count, body)

    def norm_back(source_ref, gain, grad_normed_ref):
        def body(rows):
            centred, scale = row_stats(source_ref[rows, :])
            unit = centred * scale
            grad_normed = grad_normed_ref[rows, :]
            e = grad_normed * gains_ref[gain : gain + 1, :]
            mean = jnp.mean(e, -1, keepdims=True)
            tilt = jnp.mean(e * unit, -1, keepdims=True)
            stream_ref[rows, :] += scale * (e - mean - unit * tilt)
            gain_sums[gain : gain + 1, :] += jnp.sum(grad_normed * unit, 0, keepdims=True)

        by_rows(count, body)

    def exchange(index):
        return Exchange(
            here,
            swap_out.at[index % 2],
            swap_back.at[index % 2],
            swap_sent.at[index],
            swap_here.at[index],
        )

    def attention(kind, k, normed_ref, heads_ref, mixed_ref):
        total_ref[...] = jnp.zeros_like(total_ref)

        def compute(i, t):
            total_ref[...] += attend_block(
                kind,
                PATCHES // 4,
                t,
                normed_ref[...],
                weight(k, t),
                heads_ref,
                mixed_ref,
                mixed_sums,
                bias_ref,
            )

        return compute

    def attention_back(kind, k, normed_ref, heads_ref, mixed_ref):
        total_ref[...] = jnp.zeros_like(total_ref)

        def compute(i, t):
            step = (CHUNKS - 1 - k) * STEPS + i
            out = begin(step)
            total_ref[...] += attend_back_block(
                kind,
                PATCHES // 4,
                heads_ref.at[t],
                mixed_ref.at[t],
                low_ref,
                normed_ref,
                weight(k, t),
                grad_mixed,
                sums,
                grad_heads,
                bias_ref,
            )
            if k:
                fetch(k - 1, t).start()
            out[:, : 3 * width] = mm(normed_ref[...], grad_heads[...], TN).astype(BF16)
            out[:, 3 * width :] = mm(low_ref[...], mixed_ref[t], TN).astype(BF16)
            emit(step)

        return compute

    gain_parts[0, own_row] = gain_out[0]

    def gain_copy(r):
        flips = {"y": r // 4, "x": r // 2 % 2, "c": r % 2}
        return remote(
            gain_out.at[0],
            gain_parts.at[0, own_row],
            gain_sent.at[0, r],
            gain_here.at[0, r],
            moved(here, **flips),
        )

    for r in range(1, 8):
        gain_copy(r).start()
    for k in range(CHUNKS):
        stored(k).start()
    follow(("go",))
    loads[7].wait()

    def unit_rows(rows):
        centred, scale = row_stats(tokens_ref[rows, :])
        rows_ref[rows, :] = centred * scale

    by_rows(count, unit_rows)
    for r in range(1, 8):
        gain_copy(r).wait()
    for d in range(8):
        gains_ref[:, d * own_gains : (d + 1) * own_gains] = gain_parts[0, d, :, :own_gains]

    def scale_rows(rows):
        rows_ref[rows, :] = rows_ref[rows, :] * gains_ref[0:1, :]

    by_rows(count, scale_rows)
    swap = exchange(0)
    swap.send_frames(rows_ref)
    follow(("ln0",))
    loads[8].wait()

    def mask_rows(rows):
        stream_ref[rows, :] = stream_ref[rows, :] * live
        low_ref[rows, :] = stream_ref[rows, :].astype(BF16)

    by_rows(count, mask_rows)
    bias_ref[...] = key_bias(0, count, None, PATCHES // 4)
    gain_sums[...] = jnp.zeros_like(gain_sums)
    follow(("mask",))
    swap.take_patches(rows_ref)
    normed_time_ref[...] = rows_ref[...].astype(BF16)
    for k in range(CHUNKS):
        stored(k).wait()
    follow(("takeE0",))

    ready(0)
    loop("P0", attention("time", 0, normed_time_ref, time_heads_ref, time_mixed_ref))
    swap = exchange(1)
    swap.send_patches(total_ref)
    follow(("exch1",))
    swap.take_frames(rows_ref)
    after_time_ref[...] = tokens_ref[...] + rows_ref[...]
    layer_norm(after_time_ref, 1, normed_space_ref)
    follow(("ln1",))

    ready(1)
    loop("P1", attention("space", 1, normed_space_ref, space_heads_ref, space_mixed_ref))
    after_space_ref[...] = after_time_ref[...] + total_ref[...]
    layer_norm(after_space_ref, 2, normed_mlp_ref)
    follow(("ln2",))

    ready(2)

    def up(i, t):
        out = begin(i)
        pre_act = mm(normed_mlp_ref[...], weight(2, t)[...])
        cdf = 0.5 * (1.0 + lax.erf(pre_act * 0.5**0.5))
        hidden_ref[t] = (pre_act * cdf).astype(BF16)
        density = jnp.exp(-0.5 * pre_act * pre_act) * (0.5 / math.pi) ** 0.5
        slope_ref[t] = (cdf + pre_act * density).astype(BF16)
        out[...] = mm(low_ref[...], hidden_ref[t], TN).astype(BF16)
        emit(i)

    loop("up", up)
    ready(3)
    out_ref[...] = after_space_ref[...]

    def down(i, t):
        out_ref[...] += mm(hidden_ref[t], weight(3, t)[...], NT)
        grad_hidden = mm(low_ref[...], held[t])
        slope_ref[t] = (grad_hidden * slope_ref[t].astype(F32)).astype(BF16)
        fetch(2, t).start()

    loop("dn", down)
    out_ref[...] = out_ref[...] * live
    total_ref[...] = jnp.zeros_like(total_ref)

    def up_back(i, t):
        step = STEPS + i
        out = begin(step)
        total_ref[...] += mm(slope_ref[t], weight(2, t)[...], NT)
        fetch(1, t).start()
        out[...] = mm(normed_mlp_ref[...], slope_ref[t], TN).astype(BF16)
        emit(step)

    loop("B1", up_back)
    norm_back(after_space_ref, 2, total_ref)
    low_ref[...] = stream_ref[...].astype(BF16)
    follow(("nb2",))
    loop("B2", attention_back("space", 1, normed_space_ref, space_heads_ref, space_mixed_ref))
    norm_back(after_time_ref, 1, total_ref)
    swap = exchange(2)
    swap.send_frames(stream_ref)
    follow(("nb1",))
    swap.take_patches(rows_ref)
    low_ref[...] = rows_ref[...].astype(BF16)
    follow(("takeE2",))
    loop("B3", attention_back("time", 0, normed_time_ref, time_heads_ref, time_mixed_ref))
    swap = exchange(3)
    swap.send_patches(total_ref)
    follow(("exch3",))
    swap.take_frames(rows_ref)
    norm_back(tokens_ref, 0, rows_ref)

    line_index = here["s"] * 2 + here["h"]

    def gain_line_copy(j):
        return remote(
            gain_sums,
            gain_line.at[line_index],
            gain_sent.at[1, j],
            gain_here.at[1, j],
            moved(here, s=j // 2, h=j % 2),
        )

    def gain_back(r):
        flips = {"y": r // 4, "x": r // 2 % 2, "c": r % 2}
        return remote(
            gain_out.at[dp_row(here, **flips)],
            gain_parts.at[1, own_row],
            gain_sent.at[2, r],
            gain_here.at[2, r],
            moved(here, **flips),
        )

    for j in range(1, 4):
        gain_line_copy(j).start()
    gain_line[line_index] = gain_sums[...]
    follow(("nb0",))
    for j in range(1, 4):
        gain_line_copy(j).wait()
    total = gain_line[0] + gain_line[1] + gain_line[2] + gain_line[3]
    for d in range(8):
        gain_out[d, :, :own_gains] = total[:, d * own_gains : (d + 1) * own_gains]
    for r in range(1, 8):
        gain_back(r).start()
    gain_parts[1, own_row] = gain_out[own_row]
    follow(("gain",))
    for r in range(1, 8):
        gain_back(r).wait()
    total = gain_parts[1, 0]
    for d in range(1, 8):
        total = total + gain_parts[1, d]
    own_gain_ref[...] = total

    for k in range(CHUNKS):
        for sem in range(8):
            for j in range(4):
                if sem or j:
                    slot = slot_of(k, 0, own_row)
                    remote(
                        slot,
                        slot,
                        piece_sent.at[k, sem, j],
                        piece_here.at[k, 0, 0, 0],
                        moved(here, c=1),
                    ).wait_send()
    for step in range(last + 1):
        if step > last - 2:
            for quad in range(4):
                core_copy(step, quad).wait_send()
        for half in range(2):
            first_copy(step, half).wait_send()
            second_copy(step, half).wait_send()
        if BLOCK_ORDER[step % STEPS]:
            third_copy(step).wait_send()


def layer(live_clips, tokens, cotangent, norm_gains, *weights):
    count, columns = tokens.shape
    rows, lanes = weights[4].shape
    half = lanes // 2
    width, steps = lanes // 4, CHUNKS * STEPS
    here = pl.BlockSpec(memory_space=pltpu.VMEM)
    there = pl.BlockSpec(memory_space=pl.ANY)
    outputs = (
        shaped(CHUNKS, STEPS, columns, lanes),
        shaped(count, columns, dtype=F32),
        shaped(count, columns, dtype=F32),
        shaped(CHUNKS, rows, lanes, dtype=F32),
        shaped(8, 128, dtype=F32),
    )
    return pl.pallas_call(
        layer_kernel,
        in_specs=[pl.BlockSpec(memory_space=pltpu.SMEM)] + [there] * 9,
        out_specs=[there] + [here] * (len(outputs) - 1),
        out_shape=outputs,
        scratch_shapes=[
            pltpu.VMEM((count, columns), F32),
            pltpu.VMEM(norm_gains.shape, BF16),
            *[pltpu.VMEM(w.shape, BF16) for w in weights[:4]],
            pltpu.VMEM((CHUNKS, rows, lanes), BF16),
            pltpu.VMEM((STEPS, columns, lanes), BF16),
            pltpu.VMEM((count, columns), BF16),
            pltpu.VMEM((STEPS, count, 3 * width), BF16),
            pltpu.VMEM((STEPS, count, width), BF16),
            pltpu.VMEM((count, columns), F32),
            pltpu.VMEM((count, columns), BF16),
            pltpu.VMEM((STEPS, count, 3 * width), BF16),
            pltpu.VMEM((STEPS, count, width), BF16),
            pltpu.VMEM((count, columns), F32),
            pltpu.VMEM((count, columns), BF16),
            pltpu.VMEM((STEPS, count, lanes), BF16),
            pltpu.VMEM((STEPS, count, lanes), BF16),
            pltpu.VMEM((count, columns), BF16),
            pltpu.VMEM((count, columns), F32),
            pltpu.VMEM((count, columns), F32),
            pltpu.VMEM((count, width), F32),
            pltpu.VMEM((count, 3 * width), F32),
            pltpu.VMEM((count, width), BF16),
            pltpu.VMEM((count, 3 * width), BF16),
            pltpu.VMEM((count, count), F32),
            pltpu.VMEM((2, columns, lanes), BF16),
            pltpu.VMEM((steps, 4, 2, rows, half), BF16),
            pltpu.VMEM((4, 4, rows, lanes), BF16),
            pltpu.VMEM((steps, 2, 2, rows, half), BF16),
            pltpu.VMEM((steps, 2, rows, half), BF16),
            pltpu.VMEM((steps, 2, rows, half), BF16),
            pltpu.VMEM((8, columns), F32),
            pltpu.VMEM((8, columns), F32),
            pltpu.VMEM((4, 8, columns), F32),
            pltpu.VMEM((8, 8, 128), F32),
            pltpu.VMEM((2, 8, 8, 128), F32),
            pltpu.VMEM((2, 4, 2, PAD, columns), BF16),
            pltpu.VMEM((2, 4, 2, PAD, columns), BF16),
            pltpu.SemaphoreType.DMA((CHUNKS, 8, 4)),
            pltpu.SemaphoreType.DMA((CHUNKS, 2, 4, 4)),
            pltpu.SemaphoreType.DMA((2, 4)),
            pltpu.SemaphoreType.DMA((4, 4)),
            pltpu.SemaphoreType.DMA((steps, 2)),
            pltpu.SemaphoreType.DMA((steps, 2)),
            pltpu.SemaphoreType.DMA((steps, 2)),
            pltpu.SemaphoreType.DMA((steps, 2)),
            pltpu.SemaphoreType.DMA((steps,)),
            pltpu.SemaphoreType.DMA((steps,)),
            pltpu.SemaphoreType.DMA((3, 8)),
            pltpu.SemaphoreType.DMA((3, 8)),
            pltpu.SemaphoreType.DMA((4, 4)),
            pltpu.SemaphoreType.DMA((4, 4)),
            pltpu.SemaphoreType.DMA((STEPS,)),
            pltpu.SemaphoreType.DMA((CHUNKS,)),
            pltpu.SemaphoreType.DMA((9,)),
            pltpu.SemaphoreType.REGULAR,
        ],
        compiler_params=pltpu.CompilerParams(
            collective_id=0, has_side_effects=True, vmem_limit_bytes=67043328
        ),
        name="layer",
    )(live_clips, tokens, cotangent, norm_gains, *weights)[1:]


def finish_kernel(output_ref, grad_ref, own_ref, gain_ref, *outs):
    out_ref, stream_ref, gains, time_in, time_out, space_in, space_out, up, down = outs
    width = time_in.shape[2]
    out_ref[...] = output_ref[...]
    stream_ref[...] = grad_ref[...]
    gains[...] = gain_ref[: gains.shape[0], : gains.shape[1]]
    for k, into, out in ((3, time_in, time_out), (2, space_in, space_out)):
        for c in range(3):
            into[c] = own_ref[k, :, c * width : (c + 1) * width]
        out[...] = own_ref[k, :, 3 * width :].T
    up[...] = own_ref[1]
    down[...] = own_ref[0]


def finish(output, grad, own, gain, like):
    shapes = [jax.ShapeDtypeStruct(a.shape, F32) for a in like]
    here = pl.BlockSpec(memory_space=pltpu.VMEM)
    return pl.pallas_call(
        finish_kernel,
        in_specs=[here] * 4,
        out_specs=[here] * len(shapes),
        out_shape=shapes,
        name="finish",
    )(output, grad, own, gain)


def sum_gains(total, own):
    for axes in ("c", "x", "y", TENSOR):
        bit = 1
        while bit < lax.axis_size(axes):
            total = total + along(total, axes, bit)
            bit *= 2
    return lax.dynamic_slice_in_dim(total, lax.axis_index(DP) * own, own, 1)


def on_device(
    routed,
    tokens,
    live_clips,
    norm_gains,
    qkv_time,
    out_time,
    qkv_space,
    out_space,
    up_weight,
    down_weight,
    cotangent,
):
    members = lax.axis_size("c") * lax.axis_size("h")
    share = PATCHES // members
    count, columns = tokens.shape
    width = qkv_time.shape[2]
    live = jnp.where(lax.axis_index("s") < live_clips[0], 1.0, 0.0).astype(F32)

    def pack_heads(qkv, out):
        rows = qkv.shape[1]
        return jnp.concatenate([qkv.transpose(1, 0, 2).reshape(rows, -1), out.T], 1)

    if routed:
        weights = (qkv_time, out_time, qkv_space, out_space, up_weight, down_weight.T)
        done = layer(live_clips, tokens, cotangent, norm_gains, *weights)
        *found, down_own = finish(*done, (tokens, cotangent, norm_gains, *weights))
        return (*found, down_own.T)
    shards = [
        pack_heads(qkv_time, out_time),
        pack_heads(qkv_space, out_space),
        up_weight,
        down_weight.T,
    ]
    grad_stream = cotangent * live
    time_all, space_all, up_all, down_all = [gather_plain(shard) for shard in shards]
    blocks, depth, lanes = up_all.shape
    gains = lax.all_gather(norm_gains, DP, axis=1, tiled=True).astype(F32)
    normed_time = to_patches(normalize(tokens, gains[0]).astype(BF16), members)
    time_heads, time_mixed, change = attend("time", normed_time, time_all, share, BF16)
    after_time = tokens + to_frames(change, members).astype(F32)
    normed_space = normalize(after_time, gains[1]).astype(BF16)
    space_heads, space_mixed, change = attend("space", normed_space, space_all, 1, F32)
    after_space = after_time + change
    normed_mlp = normalize(after_space, gains[2]).astype(BF16)
    hidden, slope = phase(
        up_kernel,
        "up",
        (normed_mlp, up_all),
        (shaped(blocks, count, lanes), shaped(blocks, count, lanes)),
        cost=12,
    )
    (change,) = phase(
        down_kernel, "down", (hidden, down_all), (shaped(count, depth, dtype=F32),), cost=4
    )
    after_mlp = after_space + change
    grad_low = grad_stream.astype(BF16)
    work = (pltpu.VMEM((depth, lanes), BF16),)
    *down_grads, grad_pre = phase(
        down_back_kernel,
        "down_back",
        (grad_low, down_all, hidden, slope),
        (*grad_shapes(down_all, False), shaped(blocks, count, lanes)),
        work,
        cost=8,
    )
    *up_grads, grad_normed = phase(
        up_back_kernel,
        "up_back",
        (normed_mlp, up_all, grad_pre),
        (*grad_shapes(up_all, False), shaped(count, depth, dtype=F32)),
        work,
        cost=8,
    )
    grad_part, gain_mlp = norm_back(after_space, gains[2], grad_normed)
    grad_stream = grad_stream + grad_part
    space_grads, grad_normed = attend_back(
        "space",
        normed_space,
        space_all,
        space_heads,
        space_mixed,
        grad_stream.astype(BF16),
        1,
        F32,
        False,
    )
    grad_part, gain_space = norm_back(after_time, gains[1], grad_normed)
    grad_stream = grad_stream + grad_part
    grad_low = to_patches(grad_stream.astype(BF16), members)
    time_grads, grad_normed = attend_back(
        "time", normed_time, time_all, time_heads, time_mixed, grad_low, share, BF16, routed
    )
    grad_normed = to_frames(grad_normed, members).astype(F32)
    grad_part, gain_time = norm_back(tokens, gains[0], grad_normed)
    grad_tokens = grad_stream + grad_part
    down_own = reduce_plain(down_grads).T
    up_own = reduce_plain(up_grads)
    space_own = reduce_plain(space_grads)
    time_own = reduce_plain(time_grads)
    gains_own = sum_gains(jnp.stack([gain_time, gain_space, gain_mlp]), norm_gains.shape[1])
    output = after_mlp * live

    def unpack(own):
        rows = own.shape[0]
        return own[:, : 3 * width].reshape(rows, 3, width).transpose(1, 0, 2), own[:, 3 * width :].T

    time_in_own, time_out_own = unpack(time_own)
    space_in_own, space_out_own = unpack(space_own)
    return (
        output,
        grad_tokens,
        gains_own,
        time_in_own,
        time_out_own,
        space_in_own,
        space_out_own,
        up_own,
        down_own,
    )


def solution(mesh):
    n_dp, n_tensor = mesh.devices.shape

    def run(*args):
        slots = args[0].shape[0] // (n_dp * HALF * PATCHES)
        fine = Mesh(mesh.devices.reshape(n_dp // 4, 2, 2, slots, n_tensor // slots), ALL)
        in_specs = (
            P(ALL, None),
            P(DP),
            P(None, DP),
            P(None, DP, TENSOR),
            P(TENSOR, DP),
            P(None, DP, TENSOR),
            P(TENSOR, DP),
            P(DP, TENSOR),
            P(TENSOR, DP),
            P(ALL, None),
        )
        out_specs = (in_specs[0], in_specs[0]) + in_specs[2:9]
        routed = fine.devices.shape == (2, 2, 2, 2, 2)
        return jax.shard_map(
            functools.partial(on_device, routed), mesh=fine, in_specs=in_specs, out_specs=out_specs, check_vma=False
        )(*args)

    return run
```

profile of v0, /device:TPU:0, one launch (start us, length us, event | category | flops | bytes accessed | tf_op | source)
XLA Modules:
  0.0 202.1 jit_solution(981446336705836906)
XLA Ops:
  1.3 196.7 %layer.1 = (bf16[4,4,768,768]{3,2,1,0:T(8,128)(2,1)}, f32[392,768]{1,0:T(8,128)}, f32[392,768]{1,0:T(8,128)}, f32[4,96,768]{2,1,0:T(8,128)}, f32[8,128]{1,0:T(8,128)}) custom-call(s32[1]{0:T(128)S(6)} %copy.19.live_ref, f32[392,768]{1,0:T(8,128)} %tokens_hbm.1, f32[392,768]{1,0:T(8,128)} %cotangent_hbm.1, bf16[3,96]{1,0:T(4,128)(2,1)} %gain_hbm.1, ...), custom_call_target="tpu_custom_call" | custom-call | tf_op jit(solution)/shard_map/layer/pallas_call | solution.py:1194
  198.0 4.1 %finish.1 = (f32[392,768]{1,0:T(8,128)}, f32[392,768]{1,0:T(8,128)}, f32[3,96]{1,0:T(4,128)}, f32[3,96,192]{2,1,0:T(8,128)}, f32[192,96]{1,0:T(8,128)}, /*index=...) custom-call(f32[392,768]{1,0:T(8,128)} %get-tuple-element.22.output_ref, ...), custom_call_target="tpu_custom_call" | custom-call | tf_op jit(solution)/shard_map/finish/pallas_call | solution.py:1280
where the time goes:
time: 203 us; the launch traced here: 202 us
  Pallas kernels  201 us (99%)
    pallas_call x1, Pallas kernels, layer(): pl.pallas_call(layer_kernel, in_specs=[pl.BlockSpec(memory_space=pltpu.SM...  197 us
    pallas_call x1, Pallas kernels, finish(): pl.pallas_call(finish_kernel, in_specs=[here] * 4, out_specs=[here] * len...  4.1 us

commit v1 on v0

--- a/solution.py
+++ b/solution.py
@@ -432,38 +432,61 @@
                 self.device(member),
             ).wait()
 
-    def send(self, rows_ref, first_row):
+    def send(self, rows_ref, rows_of):
         share = PATCHES // 4
         for member in range(4):
             for frame in range(2):
-                low = first_row(member, frame)
-                self.out[member, frame, :share, :] = rows_ref[low : low + share, :].astype(BF16)
+                rows = rows_of(member, frame)
+                self.out[member, frame, :share, :] = rows_ref[rows, :].astype(BF16)
             self.start(member)
 
-    def take(self, rows_ref, first_row):
+    def take(self, rows_ref, rows_of):
         share = PATCHES // 4
         for member in range(4):
             self.finish(member)
             for frame in range(2):
-                low = first_row(member, frame)
-                rows_ref[low : low + share, :] = self.back[member, frame, :share, :].astype(F32)
+                rows = rows_of(member, frame)
+                rows_ref[rows, :] = self.back[member, frame, :share, :].astype(F32)
 
     @staticmethod
     def by_frame(member, frame):
-        return frame * PATCHES + member * (PATCHES // 4)
+        low = frame * PATCHES + member * (PATCHES // 4)
+        return slice(low, low + PATCHES // 4)
 
     @staticmethod
     def by_share(member, frame):
-        return (member * 2 + frame) * (PATCHES // 4)
+        return pl.ds(member * 2 + frame, PATCHES // 4, stride=FRAMES)
+
+    def parts(self, patch_ref):
+        for block in range(patch_ref.shape[0]):
+            yield block, slice(block * 128, (block + 1) * 128)
 
     def send_frames(self, rows_ref):
         self.send(rows_ref, self.by_frame)
 
-    def take_patches(self, rows_ref):
-        self.take(rows_ref, self.by_share)
-
-    def send_patches(self, rows_ref):
-        self.send(rows_ref, self.by_share)
+    def take_patches(self, patch_ref, low_ref):
+        share = PATCHES // 4
+        for member in range(4):
+            self.finish(member)
+            for frame in range(2):
+                for block, lanes in self.parts(patch_ref):
+                    patch_ref[block, self.by_share(member, frame), :] = self.back[
+                        member, frame, :share, lanes
+                    ].astype(F32)
+        for block, lanes in self.parts(patch_ref):
+            low_ref[:, lanes] = patch_ref[block].astype(BF16)
+
+    def send_patches(self, rows_ref, patch_ref):
+        share = PATCHES // 4
+        for block, lanes in self.parts(patch_ref):
+            patch_ref[block] = rows_ref[:, lanes]
+        for member in range(4):
+            for frame in range(2):
+                for block, lanes in self.parts(patch_ref):
+                    self.out[member, frame, :share, lanes] = patch_ref[
+                        block, self.by_share(member, frame), :
+                    ].astype(BF16)
+            self.start(member)
 
     def take_frames(self, rows_ref):
         self.take(rows_ref, self.by_frame)
@@ -484,58 +507,95 @@
     return centred, lax.rsqrt(spread + EPSILON)
 
 
-def attend_block(kind, stride, t, normed, weight, heads_ref, mixed_ref, sums, bias_ref):
+def attention_units(kind, count, width):
+    found = []
+    if kind == "time":
+        tile = 96
+        starts = list(range(0, count - tile, tile))
+        ends = starts[1:] + [count]
+    else:
+        starts = [low for low, size, group in windows(kind, count)]
+        ends = [low + size for low, size, group in windows(kind, count)]
+    for index, (start, end) in enumerate(zip(starts, ends)):
+        size = end - start
+        keys = row_ids((size, size), 0, 0)
+        first, final = 0, size
+        if kind == "time":
+            together = keys // FRAMES == row_ids((size, size), 1, 0) // FRAMES
+        else:
+            first = index * PATCHES - start
+            final = first + PATCHES
+            together = (keys >= first) & (keys < final)
+        bias = jnp.where(together, 0.0, -1e30)
+        found += [(start, size, first, final, bias, head) for head in range(width // HEAD_DIM)]
+    return found
+
+
+def attend_block(kind, t, normed, weight, heads_ref, mixed_ref, sums):
     count, width = mixed_ref.shape[1:]
     heads_ref[t] = mm(normed, weight[:, : 3 * width]).astype(BF16)
     heads = heads_ref.at[t]
-    sums[...] = jnp.zeros_like(sums)
-    for start, size, group in windows(kind, count):
-        bias = bias_ref[...] if group is None else key_bias(start, size, group, stride)
-        rows = pl.ds(start, size)
-        for head in range(width // HEAD_DIM):
-            low = head * HEAD_DIM
-            query, key, value = head_slices(heads, rows, width, head)
-            scores = mm(key, query * HEAD_DIM**-0.5, NT) + bias
-            weights = jnp.exp(scores - jnp.max(scores, 0, keepdims=True))
-            total = jnp.sum(weights, 0, keepdims=True)
-            blended = (mm(value.T, weights.astype(BF16)) / total).T
-            if group is not None:
-                blended = jnp.where(row_valid(start, size, group, HEAD_DIM), blended, 0.0)
-            sums[rows, low : low + HEAD_DIM] += blended
-    mixed_ref[t] = sums[...].astype(BF16)
+    target = mixed_ref.at[t] if kind == "time" else sums
+    units = attention_units(kind, count, width)
+    for batch in range(0, len(units), 6):
+        some = units[batch : batch + 6]
+        parts = [head_slices(heads, pl.ds(u[0], u[1]), width, u[5]) for u in some]
+        scores = [
+            mm(key, query * HEAD_DIM**-0.5, NT) + u[4] for u, (query, key, value) in zip(some, parts)
+        ]
+        weights = [jnp.exp(x - jnp.max(x, 0, keepdims=True)) for x in scores]
+        scales = [1.0 / jnp.sum(x, 0, keepdims=True) for x in weights]
+        blended = [
+            (mm(value.T, x.astype(BF16)) * scale).T
+            for x, scale, (query, key, value) in zip(weights, scales, parts)
+        ]
+        for (start, size, first, final, bias, head), x in zip(some, blended):
+            lanes = slice(head * HEAD_DIM, (head + 1) * HEAD_DIM)
+            target[start + first : start + final, lanes] = x[first:final].astype(target.dtype)
+    if kind != "time":
+        mixed_ref[t] = sums[...].astype(BF16)
     return mm(mixed_ref[t], weight[:, 3 * width :], NT)
 
 
-def attend_back_block(
-    kind, stride, heads, mixed, grad, normed, weight, grad_mixed, sums, grad_heads, bias_ref
-):
+def attend_back_block(kind, heads, mixed, grad, weight, grad_mixed, sums, grad_heads):
     count, width = mixed.shape
     scale = HEAD_DIM**-0.5
     grad_mixed[...] = mm(grad[...], weight[:, 3 * width :]).astype(BF16)
-    sums[...] = jnp.zeros_like(sums)
-    for start, size, group in windows(kind, count):
-        bias = bias_ref[...] if group is None else key_bias(start, size, group, stride)
-        rows = pl.ds(start, size)
-        for head in range(width // HEAD_DIM):
-            low = head * HEAD_DIM
+    target = grad_heads if kind == "time" else sums
+    units = attention_units(kind, count, width)
+    batch_size = 12 if kind == "time" else 3
+    for batch in range(0, len(units), batch_size):
+        some = units[batch : batch + batch_size]
+        parts = []
+        for start, size, first, final, bias, head in some:
+            rows = pl.ds(start, size)
             query, key, value = head_slices(heads, rows, width, head)
-            query = query * scale
-            grad_here = grad_mixed[rows, low : low + HEAD_DIM]
-            if group is not None:
-                valid = row_valid(start, size, group, HEAD_DIM)
+            grad_here = grad_mixed[rows, head * HEAD_DIM : (head + 1) * HEAD_DIM]
+            if kind != "time":
+                ids = row_ids((size, HEAD_DIM), 0, 0)
+                valid = (ids >= first) & (ids < final)
                 grad_here = jnp.where(valid, grad_here.astype(F32), 0.0).astype(BF16)
-            scores = mm(key, query, NT) + bias
-            weights = jnp.exp(scores - jnp.max(scores, 0, keepdims=True))
-            weights = weights * (1.0 / jnp.sum(weights, 0, keepdims=True))
-            grad_weights = mm(value, grad_here, NT)
-            row_terms = jnp.sum(weights * grad_weights, 0, keepdims=True)
-            grad_scores = (weights * (grad_weights - row_terms)).astype(BF16)
-            sums[rows, low : low + HEAD_DIM] += (mm(key.T, grad_scores) * scale).T
-            low += width
-            sums[rows, low : low + HEAD_DIM] += mm(grad_scores, query)
-            low += width
-            sums[rows, low : low + HEAD_DIM] += mm(weights.astype(BF16), grad_here)
-    grad_heads[...] = sums[...].astype(BF16)
+            parts.append((query * scale, key, value, grad_here))
+        scores = [mm(p[1], p[0], NT) + u[4] for u, p in zip(some, parts)]
+        grad_weights = [mm(p[2], p[3], NT) for p in parts]
+        weights = [jnp.exp(x - jnp.max(x, 0, keepdims=True)) for x in scores]
+        weights = [x * (1.0 / jnp.sum(x, 0, keepdims=True)) for x in weights]
+        grad_values = [mm(x.astype(BF16), p[3]) for x, p in zip(weights, parts)]
+        grad_scores = [
+            (x * (y - jnp.sum(x * y, 0, keepdims=True))).astype(BF16)
+            for x, y in zip(weights, grad_weights)
+        ]
+        grad_keys = [mm(x, p[0]) for x, p in zip(grad_scores, parts)]
+        grad_queries = [(mm(p[1].T, x) * scale).T for x, p in zip(grad_scores, parts)]
+        for u, *grads in zip(some, grad_queries, grad_keys, grad_values):
+            start, size, first, final, bias, head = u
+            for c, x in enumerate(grads):
+                low = c * width + head * HEAD_DIM
+                target[start + first : start + final, low : low + HEAD_DIM] = x[
+                    first:final
+                ].astype(target.dtype)
+    if kind != "time":
+        grad_heads[...] = sums[...].astype(BF16)
     return mm(grad_heads[...], weight[:, : 3 * width], NT)
 
 
@@ -543,31 +603,31 @@
 BLOCK_ORDER = (1, 2, 3, 0)
 ORDER = (
     ("go",),
-    ("zs", 0, 1), ("zs", 0, 2), ("zs", 0, 3), ("line", 0, 0), ("line", 1, 0), ("ln0",),
-    ("line", 2, 0), ("mask",), ("line", 3, 0), ("line", 0, 1), ("zs", 1, 1), ("line", 0, 2),
-    ("zs", 1, 2), ("relay", 0, 0), ("zs", 1, 3), ("line", 0, 3), ("takeE0",), ("relay", 0, 1),
-    ("zs", 2, 1), ("relay", 0, 2), ("line", 1, 1), ("zs", 2, 2), ("across", 0, 0),
-    ("relay", 1, 0), ("relay", 0, 3), ("across", 0, 2), ("zs", 2, 3), ("line", 1, 2),
-    ("across", 0, 1), ("line", 1, 3), ("zs", 3, 1), ("across", 0, 3), ("P0", 0), ("relay", 1, 1),
-    ("across", 1, 0), ("zs", 3, 2), ("P0", 1), ("relay", 1, 2), ("line", 2, 1), ("zs", 3, 3),
-    ("P0", 2), ("relay", 1, 3), ("relay", 2, 0), ("P0", 3), ("across", 1, 1), ("across", 1, 2),
-    ("line", 2, 2), ("exch1",), ("relay", 3, 0), ("line", 2, 3), ("across", 2, 0),
-    ("across", 1, 3), ("relay", 2, 1), ("relay", 2, 2), ("line", 3, 1), ("across", 3, 0),
-    ("ln1",), ("relay", 2, 3), ("line", 3, 2), ("P1", 0), ("across", 2, 1), ("across", 2, 2),
-    ("line", 3, 3), ("P1", 1), ("relay", 3, 1), ("P1", 2), ("across", 2, 3), ("P1", 3),
-    ("relay", 3, 2), ("ln2",), ("relay", 3, 3), ("up", 0), ("across", 3, 1), ("up", 1),
-    ("across", 3, 2), ("core", 0), ("up", 2), ("across", 3, 3), ("core", 1), ("up", 3),
-    ("core", 2), ("dn", 0), ("first", 0), ("core", 3), ("dn", 1), ("first", 1), ("dn", 2),
-    ("dn", 3), ("first", 2), ("B1", 0), ("second", 0), ("B1", 1), ("first", 3), ("core", 4),
-    ("B1", 2), ("second", 1), ("core", 5), ("second", 2), ("B1", 3), ("second", 3), ("nb2",),
-    ("core", 6), ("core", 7), ("B2", 0), ("first", 4), ("first", 5), ("B2", 1), ("third", 0),
-    ("first", 6), ("first", 7), ("core", 8), ("B2", 2), ("second", 4), ("second", 5),
-    ("second", 6), ("core", 9), ("B2", 3), ("second", 7), ("first", 8), ("core", 10), ("nb1",),
-    ("first", 9), ("core", 11), ("second", 8), ("first", 10), ("second", 9), ("third", 1),
-    ("first", 11), ("second", 10), ("takeE2",), ("B3", 0), ("second", 11), ("B3", 1),
-    ("core", 12), ("B3", 2), ("third", 2), ("core", 13), ("B3", 3), ("first", 12), ("core", 14),
-    ("exch3",), ("first", 13), ("core", 15), ("second", 12), ("first", 14), ("nb0",),
-    ("second", 13), ("gain",), ("first", 15), ("second", 14), ("second", 15), ("third", 3),
+    ("line", 0, 0), ("zs", 0, 1), ("line", 3, 0), ("zs", 0, 3), ("line", 1, 0), ("zs", 0, 2),
+    ("zs", 2, 3), ("ln0",), ("mask",), ("zs", 1, 2), ("line", 2, 0), ("line", 0, 3),
+    ("line", 0, 2), ("zs", 1, 1), ("line", 0, 1), ("relay", 0, 2), ("line", 2, 3), ("zs", 1, 3),
+    ("relay", 0, 1), ("relay", 0, 3), ("relay", 0, 0), ("across", 0, 1), ("line", 1, 2),
+    ("line", 1, 1), ("across", 0, 2), ("zs", 2, 2), ("across", 0, 3), ("across", 0, 0),
+    ("relay", 1, 0), ("takeE0",), ("line", 1, 3), ("relay", 2, 0), ("zs", 2, 1), ("zs", 3, 1),
+    ("P0", 0), ("relay", 1, 2), ("relay", 2, 3), ("P0", 1), ("P0", 2), ("P0", 3), ("exch1",),
+    ("relay", 1, 1), ("across", 1, 2), ("relay", 1, 3), ("line", 2, 2), ("across", 1, 1),
+    ("line", 2, 1), ("zs", 3, 2), ("across", 1, 3), ("across", 1, 0), ("line", 3, 1),
+    ("across", 2, 0), ("ln1",), ("P1", 0), ("relay", 2, 1), ("zs", 3, 3), ("relay", 2, 2),
+    ("P1", 1), ("across", 2, 3), ("line", 3, 2), ("P1", 2), ("P1", 3), ("line", 3, 3),
+    ("across", 2, 2), ("across", 2, 1), ("ln2",), ("relay", 3, 0), ("relay", 3, 1),
+    ("relay", 3, 2), ("up", 0), ("relay", 3, 3), ("up", 1), ("core", 0), ("across", 3, 2),
+    ("across", 3, 0), ("up", 2), ("core", 1), ("across", 3, 3), ("across", 3, 1), ("up", 3),
+    ("core", 2), ("dn", 0), ("dn", 1), ("first", 0), ("dn", 2), ("core", 3), ("dn", 3), ("B1", 0),
+    ("first", 1), ("first", 2), ("B1", 1), ("second", 0), ("first", 3), ("core", 4), ("B1", 2),
+    ("core", 5), ("B1", 3), ("nb2",), ("second", 1), ("core", 6), ("B2", 0), ("second", 2),
+    ("first", 4), ("first", 5), ("core", 7), ("B2", 1), ("core", 8), ("first", 6), ("second", 4),
+    ("B2", 2), ("second", 5), ("core", 9), ("B2", 3), ("nb1",), ("core", 10), ("second", 3),
+    ("first", 8), ("first", 9), ("third", 0), ("core", 11), ("second", 6), ("first", 10),
+    ("first", 7), ("second", 8), ("takeE2",), ("B3", 0), ("second", 9), ("B3", 1), ("first", 11),
+    ("core", 12), ("second", 10), ("B3", 2), ("core", 13), ("B3", 3), ("exch3",), ("first", 12),
+    ("core", 14), ("second", 11), ("second", 12), ("first", 13), ("first", 14), ("core", 15),
+    ("second", 13), ("third", 2), ("nb0",), ("second", 14), ("second", 7), ("first", 15),
+    ("gain",), ("second", 15), ("third", 1), ("third", 3),
 )
 
 
@@ -621,12 +681,12 @@
     slope_ref,
     low_ref,
     rows_ref,
+    patch_ref,
     total_ref,
     mixed_sums,
     sums,
     grad_mixed,
     grad_heads,
-    bias_ref,
     work,
     keep,
     came,
@@ -952,15 +1012,7 @@
 
         def compute(i, t):
             total_ref[...] += attend_block(
-                kind,
-                PATCHES // 4,
-                t,
-                normed_ref[...],
-                weight(k, t),
-                heads_ref,
-                mixed_ref,
-                mixed_sums,
-                bias_ref,
+                kind, t, normed_ref[...], weight(k, t), heads_ref, mixed_ref, mixed_sums
             )
 
         return compute
@@ -973,16 +1025,13 @@
             out = begin(step)
             total_ref[...] += attend_back_block(
                 kind,
-                PATCHES // 4,
                 heads_ref.at[t],
                 mixed_ref.at[t],
                 low_ref,
-                normed_ref,
                 weight(k, t),
                 grad_mixed,
                 sums,
                 grad_heads,
-                bias_ref,
             )
             if k:
                 fetch(k - 1, t).start()
@@ -1035,11 +1084,9 @@
         low_ref[rows, :] = stream_ref[rows, :].astype(BF16)
 
     by_rows(count, mask_rows)
-    bias_ref[...] = key_bias(0, count, None, PATCHES // 4)
     gain_sums[...] = jnp.zeros_like(gain_sums)
     follow(("mask",))
-    swap.take_patches(rows_ref)
-    normed_time_ref[...] = rows_ref[...].astype(BF16)
+    swap.take_patches(patch_ref, normed_time_ref)
     for k in range(CHUNKS):
         stored(k).wait()
     follow(("takeE0",))
@@ -1047,7 +1094,7 @@
     ready(0)
     loop("P0", attention("time", 0, normed_time_ref, time_heads_ref, time_mixed_ref))
     swap = exchange(1)
-    swap.send_patches(total_ref)
+    swap.send_patches(total_ref, patch_ref)
     follow(("exch1",))
     swap.take_frames(rows_ref)
     after_time_ref[...] = tokens_ref[...] + rows_ref[...]
@@ -1103,12 +1150,11 @@
     swap = exchange(2)
     swap.send_frames(stream_ref)
     follow(("nb1",))
-    swap.take_patches(rows_ref)
-    low_ref[...] = rows_ref[...].astype(BF16)
+    swap.take_patches(patch_ref, low_ref)
     follow(("takeE2",))
     loop("B3", attention_back("time", 0, normed_time_ref, time_heads_ref, time_mixed_ref))
     swap = exchange(3)
-    swap.send_patches(total_ref)
+    swap.send_patches(total_ref, patch_ref)
     follow(("exch3",))
     swap.take_frames(rows_ref)
     norm_back(tokens_ref, 0, rows_ref)
@@ -1215,12 +1261,12 @@
             pltpu.VMEM((STEPS, count, lanes), BF16),
             pltpu.VMEM((count, columns), BF16),
             pltpu.VMEM((count, columns), F32),
+            pltpu.VMEM((columns // 128, count, 128), F32),
             pltpu.VMEM((count, columns), F32),
             pltpu.VMEM((count, width), F32),
             pltpu.VMEM((count, 3 * width), F32),
             pltpu.VMEM((count, width), BF16),
             pltpu.VMEM((count, 3 * width), BF16),
-            pltpu.VMEM((count, count), F32),
             pltpu.VMEM((2, columns, lanes), BF16),
             pltpu.VMEM((steps, 4, 2, rows, half), BF16),
             pltpu.VMEM((4, 4, rows, lanes), BF16),

time: 203 us -> 188 us (0.926)
  Pallas kernels: 201 us -> 186 us
    pallas_call x1, Pallas kernels: 197 us -> 182 us  [layer(): pl.pallas_call(layer_kernel, in_specs=[pl.BlockSpec(memory_space=pltpu.SM...]
where the time goes in v1:
time: 188 us
  Pallas kernels  186 us (99%)
    pallas_call x1, Pallas kernels, layer(): pl.pallas_call(layer_kernel, in_specs=[pl.BlockSpec(memory_space=pltpu.SM...  182 us
    pallas_call x1, Pallas kernels, finish(): pl.pallas_call(finish_kernel, in_specs=[here] * 4, out_specs=[here] * len...  4.1 us

profile of v1, /device:TPU:0, one launch (start us, length us, event | category | flops | bytes accessed | tf_op | source)
XLA Modules:
  0.0 187.6 jit_solution(15076454161458358960)
XLA Ops:
  1.3 182.2 %layer.1 = (bf16[4,4,768,768]{3,2,1,0:T(8,128)(2,1)}, f32[392,768]{1,0:T(8,128)}, f32[392,768]{1,0:T(8,128)}, f32[4,96,768]{2,1,0:T(8,128)}, f32[8,128]{1,0:T(8,128)}) custom-call(s32[1]{0:T(128)S(6)} %copy.19.live_ref, f32[392,768]{1,0:T(8,128)} %tokens_hbm.1, f32[392,768]{1,0:T(8,128)} %cotangent_hbm.1, bf16[3,96]{1,0:T(4,128)(2,1)} %gain_hbm.1, ...), custom_call_target="tpu_custom_call" | custom-call | tf_op jit(solution)/shard_map/layer/pallas_call | solution.py:1240
  183.5 4.1 %finish.1 = (f32[392,768]{1,0:T(8,128)}, f32[392,768]{1,0:T(8,128)}, f32[3,96]{1,0:T(4,128)}, f32[3,96,192]{2,1,0:T(8,128)}, f32[192,96]{1,0:T(8,128)}, /*index=...) custom-call(f32[392,768]{1,0:T(8,128)} %get-tuple-element.22.output_ref, ...), custom_call_target="tpu_custom_call" | custom-call | tf_op jit(solution)/shard_map/finish/pallas_call | solution.py:1326

commit v2 on v1

--- a/solution.py
+++ b/solution.py
@@ -603,31 +603,31 @@
 BLOCK_ORDER = (1, 2, 3, 0)
 ORDER = (
     ("go",),
-    ("line", 0, 0), ("zs", 0, 1), ("line", 3, 0), ("zs", 0, 3), ("line", 1, 0), ("zs", 0, 2),
-    ("zs", 2, 3), ("ln0",), ("mask",), ("zs", 1, 2), ("line", 2, 0), ("line", 0, 3),
-    ("line", 0, 2), ("zs", 1, 1), ("line", 0, 1), ("relay", 0, 2), ("line", 2, 3), ("zs", 1, 3),
-    ("relay", 0, 1), ("relay", 0, 3), ("relay", 0, 0), ("across", 0, 1), ("line", 1, 2),
-    ("line", 1, 1), ("across", 0, 2), ("zs", 2, 2), ("across", 0, 3), ("across", 0, 0),
-    ("relay", 1, 0), ("takeE0",), ("line", 1, 3), ("relay", 2, 0), ("zs", 2, 1), ("zs", 3, 1),
-    ("P0", 0), ("relay", 1, 2), ("relay", 2, 3), ("P0", 1), ("P0", 2), ("P0", 3), ("exch1",),
-    ("relay", 1, 1), ("across", 1, 2), ("relay", 1, 3), ("line", 2, 2), ("across", 1, 1),
-    ("line", 2, 1), ("zs", 3, 2), ("across", 1, 3), ("across", 1, 0), ("line", 3, 1),
-    ("across", 2, 0), ("ln1",), ("P1", 0), ("relay", 2, 1), ("zs", 3, 3), ("relay", 2, 2),
-    ("P1", 1), ("across", 2, 3), ("line", 3, 2), ("P1", 2), ("P1", 3), ("line", 3, 3),
-    ("across", 2, 2), ("across", 2, 1), ("ln2",), ("relay", 3, 0), ("relay", 3, 1),
-    ("relay", 3, 2), ("up", 0), ("relay", 3, 3), ("up", 1), ("core", 0), ("across", 3, 2),
-    ("across", 3, 0), ("up", 2), ("core", 1), ("across", 3, 3), ("across", 3, 1), ("up", 3),
-    ("core", 2), ("dn", 0), ("dn", 1), ("first", 0), ("dn", 2), ("core", 3), ("dn", 3), ("B1", 0),
-    ("first", 1), ("first", 2), ("B1", 1), ("second", 0), ("first", 3), ("core", 4), ("B1", 2),
-    ("core", 5), ("B1", 3), ("nb2",), ("second", 1), ("core", 6), ("B2", 0), ("second", 2),
-    ("first", 4), ("first", 5), ("core", 7), ("B2", 1), ("core", 8), ("first", 6), ("second", 4),
-    ("B2", 2), ("second", 5), ("core", 9), ("B2", 3), ("nb1",), ("core", 10), ("second", 3),
-    ("first", 8), ("first", 9), ("third", 0), ("core", 11), ("second", 6), ("first", 10),
-    ("first", 7), ("second", 8), ("takeE2",), ("B3", 0), ("second", 9), ("B3", 1), ("first", 11),
-    ("core", 12), ("second", 10), ("B3", 2), ("core", 13), ("B3", 3), ("exch3",), ("first", 12),
-    ("core", 14), ("second", 11), ("second", 12), ("first", 13), ("first", 14), ("core", 15),
-    ("second", 13), ("third", 2), ("nb0",), ("second", 14), ("second", 7), ("first", 15),
-    ("gain",), ("second", 15), ("third", 1), ("third", 3),
+    ("zs", 0, 2), ("line", 2, 0), ("line", 1, 0), ("zs", 0, 1), ("line", 0, 0), ("zs", 0, 3),
+    ("line", 0, 2), ("line", 0, 1), ("relay", 0, 0), ("zs", 1, 2), ("relay", 0, 2),
+    ("line", 0, 3), ("zs", 1, 3), ("line", 1, 2), ("zs", 1, 1), ("ln0",), ("across", 0, 0),
+    ("relay", 0, 3), ("relay", 0, 1), ("across", 0, 2), ("relay", 1, 0), ("zs", 2, 1),
+    ("zs", 2, 3), ("zs", 2, 2), ("mask",), ("relay", 1, 2), ("across", 0, 1), ("across", 0, 3),
+    ("line", 1, 3), ("zs", 3, 3), ("line", 1, 1), ("line", 2, 1), ("takeE0",), ("relay", 1, 3),
+    ("P0", 0), ("relay", 1, 1), ("P0", 1), ("line", 2, 3), ("P0", 2), ("P0", 3), ("line", 2, 2),
+    ("exch1",), ("relay", 2, 0), ("across", 1, 0), ("relay", 2, 1), ("relay", 2, 3),
+    ("line", 3, 0), ("zs", 3, 1), ("across", 1, 3), ("across", 1, 1), ("relay", 2, 2),
+    ("line", 3, 3), ("across", 1, 2), ("zs", 3, 2), ("ln1",), ("P1", 0), ("P1", 1),
+    ("line", 3, 1), ("P1", 2), ("across", 2, 3), ("across", 2, 0), ("across", 2, 1),
+    ("across", 2, 2), ("line", 3, 2), ("P1", 3), ("relay", 3, 0), ("ln2",), ("relay", 3, 3),
+    ("up", 0), ("relay", 3, 1), ("relay", 3, 2), ("up", 1), ("core", 0), ("across", 3, 3),
+    ("across", 3, 0), ("up", 2), ("core", 1), ("across", 3, 2), ("across", 3, 1), ("up", 3),
+    ("core", 2), ("first", 0), ("dn", 0), ("dn", 1), ("dn", 2), ("dn", 3), ("first", 1),
+    ("B1", 0), ("core", 3), ("B1", 1), ("second", 0), ("first", 2), ("core", 4), ("second", 1),
+    ("B1", 2), ("core", 5), ("B1", 3), ("nb2",), ("first", 4), ("second", 2), ("core", 6),
+    ("B2", 0), ("first", 5), ("core", 7), ("second", 4), ("B2", 1), ("core", 8), ("B2", 2),
+    ("first", 6), ("core", 9), ("second", 5), ("B2", 3), ("nb1",), ("core", 10), ("first", 9),
+    ("second", 6), ("first", 3), ("first", 10), ("first", 8), ("core", 11), ("first", 7),
+    ("second", 9), ("takeE2",), ("B3", 0), ("second", 10), ("B3", 1), ("second", 8), ("core", 12),
+    ("B3", 2), ("core", 13), ("B3", 3), ("first", 12), ("exch3",), ("second", 3), ("core", 14),
+    ("first", 13), ("second", 12), ("core", 15), ("first", 14), ("first", 11), ("second", 13),
+    ("third", 0), ("second", 7), ("nb0",), ("second", 14), ("first", 15), ("second", 11),
+    ("third", 2), ("third", 1), ("gain",), ("second", 15), ("third", 3),
 )
 
 
@@ -641,6 +641,8 @@
     return found
 
 
+LINE_ACROSS = ()
+SUM_ACROSS = (0, 1)
 AFTER = after_each(ORDER)
 
 
@@ -656,6 +658,10 @@
     up_hbm,
     down_hbm,
     weight_ref,
+    out_hbm,
+    stream_hbm,
+    own_hbm,
+    own_gain_hbm,
     out_ref,
     stream_ref,
     own_ref,
@@ -693,6 +699,7 @@
     first,
     second,
     third,
+    fourth,
     gains_ref,
     gain_sums,
     gain_line,
@@ -710,6 +717,8 @@
     second_here,
     third_sent,
     third_here,
+    fourth_sent,
+    fourth_here,
     gain_sent,
     gain_here,
     swap_sent,
@@ -717,6 +726,7 @@
     held_sem,
     own_sem,
     load_sem,
+    store_sem,
     credit,
 ):
     here = place()
@@ -742,6 +752,14 @@
             )
         )
     ]
+    stores = [
+        pltpu.make_async_copy(source, target, store_sem.at[i])
+        for i, (source, target) in enumerate(
+            [(out_ref, out_hbm), (stream_ref, stream_hbm)]
+            + [(own_ref.at[k], own_hbm.at[k]) for k in range(CHUNKS)]
+            + [(own_gain_ref, own_gain_hbm)]
+        )
+    ]
     greet(here, "call")
     for load in loads:
         load.start()
@@ -802,11 +820,13 @@
         spread(piece(k, j, 0) if j else shard_ref.at[k], k, j)
 
     def relay(k, j):
-        up = j // 2
         arrived(k, 0, 1, j)
         send(piece(k, j, 1), k, j, 1, 5, 1, 1, c=1)
         arrived(k, 0, 2, j)
         send(piece(k, j, 2), k, j, 2, 6, 1, 2, c=1)
+        if j == 1 and k in LINE_ACROSS:
+            return
+        up = (j // 2 + k) % 2
         source = slot_of(k, j, dp_row(here, y=up, x=1 - up))
         remote(
             source,
@@ -819,6 +839,14 @@
     def across(k, j):
         arrived(k, 0, 3, j)
         send(piece(k, j, 3), k, j, 3, 7, 1, 3, c=1)
+        if j == 0 and k in LINE_ACROSS:
+            remote(
+                piece(k, 0, 3),
+                piece(k, 1, 3),
+                piece_sent.at[k, 3, 1],
+                piece_here.at[k, 0, 3, 1],
+                moved(here, h=1),
+            ).start()
 
     def fetch(k, t):
         return pltpu.make_async_copy(weight_ref.at[k, t], held.at[t], held_sem.at[t])
@@ -853,13 +881,26 @@
             moved(here, c=1),
         )
 
+    def quads_sent(step):
+        return 1 if BLOCK_ORDER[step % STEPS] == 1 and step // STEPS in SUM_ACROSS else 2
+
     def first_copy(step, half):
+        quads = quads_sent(step)
         return remote(
-            keep.at[step, pl.ds(2, 2), half],
-            first.at[step, half],
+            keep.at[step, pl.ds(2, quads), half],
+            first.at[step, half, pl.ds(0, quads)],
             first_sent.at[step, half],
             first_here.at[step, half],
             moved(here, y=1 - half, x=half),
+        )
+
+    def fourth_copy(index):
+        return remote(
+            keep.at[index * STEPS + BLOCK_ORDER.index(1), 3],
+            fourth.at[index],
+            fourth_sent.at[index],
+            fourth_here.at[index],
+            moved(here, h=1),
         )
 
     def second_copy(step, half):
@@ -898,6 +939,7 @@
             core_copy(step, quad).start()
 
     def take_core(step):
+        block = BLOCK_ORDER[step % STEPS]
         for quad in range(4):
             core_copy(step, quad).wait_recv()
         for index in (2, 3, 1, 0):
@@ -906,9 +948,15 @@
                 lanes = slice(half * half_lanes, (half + 1) * half_lanes)
                 own = work[step % 2, grad_rows(0, quad), lanes].astype(F32)
                 both = own + came[step % 4, quad, :, lanes].astype(F32)
+                if index == 3 and block == 0 and step // STEPS in SUM_ACROSS:
+                    if half == 0:
+                        fourth_copy(step // STEPS).wait_recv()
+                    both = both + fourth[step // STEPS, half].astype(F32)
                 keep[step, index, half] = both.astype(BF16)
-                if index == 3:
+                if index == 1 + quads_sent(step):
                     first_copy(step, half).start()
+            if index == 3 and block == 1 and step // STEPS in SUM_ACROSS:
+                fourth_copy(step // STEPS).start()
         if step <= last - 4:
             pl.semaphore_signal(
                 credit,
@@ -921,8 +969,9 @@
         for half in range(2):
             first_copy(step, half).wait_recv()
             for index in (1, 0):
-                both = keep[step, index, half].astype(F32) + first[step, half, index].astype(F32)
-                keep[step, index, half] = both.astype(BF16)
+                if index < quads_sent(step):
+                    both = keep[step, index, half].astype(F32) + first[step, half, index].astype(F32)
+                    keep[step, index, half] = both.astype(BF16)
                 if index:
                     second_copy(step, half).start()
 
@@ -945,6 +994,7 @@
                 source = third[step, half] if BLOCK_ORDER[step % STEPS] else keep[step, 0, half]
                 total = total + source.astype(F32)
             own_ref[index, :, half * half_lanes : (half + 1) * half_lanes] = total
+        stores[2 + index].start()
 
     events = {
         "zs": along_line,
@@ -1131,6 +1181,7 @@
 
     loop("dn", down)
     out_ref[...] = out_ref[...] * live
+    stores[0].start()
     total_ref[...] = jnp.zeros_like(total_ref)
 
     def up_back(i, t):
@@ -1158,47 +1209,50 @@
     follow(("exch3",))
     swap.take_frames(rows_ref)
     norm_back(tokens_ref, 0, rows_ref)
+    stores[1].start()
 
     line_index = here["s"] * 2 + here["h"]
-
-    def gain_line_copy(j):
-        return remote(
-            gain_sums,
-            gain_line.at[line_index],
-            gain_sent.at[1, j],
-            gain_here.at[1, j],
-            moved(here, s=j // 2, h=j % 2),
-        )
 
     def gain_back(r):
         flips = {"y": r // 4, "x": r // 2 % 2, "c": r % 2}
         return remote(
             gain_out.at[dp_row(here, **flips)],
             gain_parts.at[1, own_row],
-            gain_sent.at[2, r],
-            gain_here.at[2, r],
+            gain_sent.at[1, r],
+            gain_here.at[1, r],
             moved(here, **flips),
         )
 
-    for j in range(1, 4):
-        gain_line_copy(j).start()
-    gain_line[line_index] = gain_sums[...]
-    follow(("nb0",))
-    for j in range(1, 4):
-        gain_line_copy(j).wait()
-    total = gain_line[0] + gain_line[1] + gain_line[2] + gain_line[3]
+    def gain_line_copy(j):
+        return remote(
+            own_gain_ref,
+            gain_line.at[line_index],
+            gain_sent.at[2, j],
+            gain_here.at[2, j],
+            moved(here, s=j // 2, h=j % 2),
+        )
+
+    total = gain_sums[...]
     for d in range(8):
         gain_out[d, :, :own_gains] = total[:, d * own_gains : (d + 1) * own_gains]
     for r in range(1, 8):
         gain_back(r).start()
     gain_parts[1, own_row] = gain_out[own_row]
-    follow(("gain",))
+    follow(("nb0",))
     for r in range(1, 8):
         gain_back(r).wait()
     total = gain_parts[1, 0]
     for d in range(1, 8):
         total = total + gain_parts[1, d]
     own_gain_ref[...] = total
+    for j in range(1, 4):
+        gain_line_copy(j).start()
+    gain_line[line_index] = total
+    follow(("gain",))
+    for j in range(1, 4):
+        gain_line_copy(j).wait()
+    own_gain_ref[...] = gain_line[0] + gain_line[1] + gain_line[2] + gain_line[3]
+    stores[2 + CHUNKS].start()
 
     for k in range(CHUNKS):
         for sem in range(8):
@@ -1221,6 +1275,10 @@
             second_copy(step, half).wait_send()
         if BLOCK_ORDER[step % STEPS]:
             third_copy(step).wait_send()
+    for index in SUM_ACROSS:
+        fourth_copy(index).wait_send()
+    for store in stores:
+        store.wait()
 
 
 def layer(live_clips, tokens, cotangent, norm_gains, *weights):
@@ -1228,7 +1286,6 @@
     rows, lanes = weights[4].shape
     half = lanes // 2
     width, steps = lanes // 4, CHUNKS * STEPS
-    here = pl.BlockSpec(memory_space=pltpu.VMEM)
     there = pl.BlockSpec(memory_space=pl.ANY)
     outputs = (
         shaped(CHUNKS, STEPS, columns, lanes),
@@ -1240,9 +1297,13 @@
     return pl.pallas_call(
         layer_kernel,
         in_specs=[pl.BlockSpec(memory_space=pltpu.SMEM)] + [there] * 9,
-        out_specs=[there] + [here] * (len(outputs) - 1),
+        out_specs=[there] * len(outputs),
         out_shape=outputs,
         scratch_shapes=[
+            pltpu.VMEM((count, columns), F32),
+            pltpu.VMEM((count, columns), F32),
+            pltpu.VMEM((CHUNKS, rows, lanes), F32),
+            pltpu.VMEM((8, 128), F32),
             pltpu.VMEM((count, columns), F32),
             pltpu.VMEM(norm_gains.shape, BF16),
             *[pltpu.VMEM(w.shape, BF16) for w in weights[:4]],
@@ -1273,9 +1334,10 @@
             pltpu.VMEM((steps, 2, 2, rows, half), BF16),
             pltpu.VMEM((steps, 2, rows, half), BF16),
             pltpu.VMEM((steps, 2, rows, half), BF16),
+            pltpu.VMEM((CHUNKS, 2, rows, half), BF16),
             pltpu.VMEM((8, columns), F32),
             pltpu.VMEM((8, columns), F32),
-            pltpu.VMEM((4, 8, columns), F32),
+            pltpu.VMEM((4, 8, 128), F32),
             pltpu.VMEM((8, 8, 128), F32),
             pltpu.VMEM((2, 8, 8, 128), F32),
             pltpu.VMEM((2, 4, 2, PAD, columns), BF16),
@@ -1290,6 +1352,8 @@
             pltpu.SemaphoreType.DMA((steps, 2)),
             pltpu.SemaphoreType.DMA((steps,)),
             pltpu.SemaphoreType.DMA((steps,)),
+            pltpu.SemaphoreType.DMA((CHUNKS,)),
+            pltpu.SemaphoreType.DMA((CHUNKS,)),
             pltpu.SemaphoreType.DMA((3, 8)),
             pltpu.SemaphoreType.DMA((3, 8)),
             pltpu.SemaphoreType.DMA((4, 4)),
@@ -1297,6 +1361,7 @@
             pltpu.SemaphoreType.DMA((STEPS,)),
             pltpu.SemaphoreType.DMA((CHUNKS,)),
             pltpu.SemaphoreType.DMA((9,)),
+            pltpu.SemaphoreType.DMA((3 + CHUNKS,)),
             pltpu.SemaphoreType.REGULAR,
         ],
         compiler_params=pltpu.CompilerParams(
@@ -1306,28 +1371,49 @@
     )(live_clips, tokens, cotangent, norm_gains, *weights)[1:]
 
 
-def finish_kernel(output_ref, grad_ref, own_ref, gain_ref, *outs):
-    out_ref, stream_ref, gains, time_in, time_out, space_in, space_out, up, down = outs
+def finish_kernel(output_hbm, grad_hbm, own_hbm, gain_ref, *rest):
+    targets, buffers, own_ref, load_sem, store_sem = rest[:9], rest[9:18], *rest[18:]
+    output, grad, gains, time_in, time_out, space_in, space_out, up, down = buffers
     width = time_in.shape[2]
-    out_ref[...] = output_ref[...]
-    stream_ref[...] = grad_ref[...]
+    sources = [(own_hbm.at[k], into) for k, into in ((0, down), (1, up))]
+    sources += [(own_hbm.at[k], own_ref.at[k - 2]) for k in (2, 3)]
+    sources += [(output_hbm, output), (grad_hbm, grad)]
+    loads = [pltpu.make_async_copy(*pair, load_sem.at[i]) for i, pair in enumerate(sources)]
+    stores = [
+        pltpu.make_async_copy(*pair, store_sem.at[i]) for i, pair in enumerate(zip(buffers, targets))
+    ]
+    for i in (2, 3, 0, 1, 4, 5):
+        loads[i].start()
     gains[...] = gain_ref[: gains.shape[0], : gains.shape[1]]
-    for k, into, out in ((3, time_in, time_out), (2, space_in, space_out)):
+    stores[2].start()
+    for k, load, into, out, low in ((0, 2, space_in, space_out, 5), (1, 3, time_in, time_out, 3)):
+        loads[load].wait()
         for c in range(3):
             into[c] = own_ref[k, :, c * width : (c + 1) * width]
+        stores[low].start()
         out[...] = own_ref[k, :, 3 * width :].T
-    up[...] = own_ref[1]
-    down[...] = own_ref[0]
+        stores[low + 1].start()
+    for load, store in ((0, 8), (1, 7), (4, 0), (5, 1)):
+        loads[load].wait()
+        stores[store].start()
+    for store in stores:
+        store.wait()
 
 
 def finish(output, grad, own, gain, like):
     shapes = [jax.ShapeDtypeStruct(a.shape, F32) for a in like]
-    here = pl.BlockSpec(memory_space=pltpu.VMEM)
+    there = pl.BlockSpec(memory_space=pl.ANY)
     return pl.pallas_call(
         finish_kernel,
-        in_specs=[here] * 4,
-        out_specs=[here] * len(shapes),
+        in_specs=[there] * 3 + [pl.BlockSpec(memory_space=pltpu.VMEM)],
+        out_specs=[there] * len(shapes),
         out_shape=shapes,
+        scratch_shapes=[
+            *[pltpu.VMEM(a.shape, F32) for a in like],
+            pltpu.VMEM((2,) + own.shape[1:], F32),
+            pltpu.SemaphoreType.DMA((6,)),
+            pltpu.SemaphoreType.DMA((len(shapes),)),
+        ],
         name="finish",
     )(output, grad, own, gain)
 

time: 188 us -> 186 us (0.989)
  Pallas kernels: 186 us -> 184 us
    pallas_call x1, Pallas kernels: 182 us -> 180 us  [layer(): pl.pallas_call(layer_kernel, in_specs=[pl.BlockSpec(memory_space=pltpu.SM...]
where the time goes in v2:
time: 186 us; the launch traced here: 185 us
  Pallas kernels  184 us (99%)
    pallas_call x1, Pallas kernels, layer(): pl.pallas_call(layer_kernel, in_specs=[pl.BlockSpec(memory_space=pltpu.SM...  180 us
    pallas_call x1, Pallas kernels, finish(): pl.pallas_call(finish_kernel, in_specs=[there] * 3 + [pl.BlockSpec(memory...  3.88 us

profile of v2, /device:TPU:0, one launch (start us, length us, event | category | flops | bytes accessed | tf_op | source)
XLA Modules:
  0.0 185.1 jit_solution(14925708210280138488)
XLA Ops:
  1.3 179.7 %layer.1 = (bf16[4,4,768,768]{3,2,1,0:T(8,128)(2,1)}, f32[392,768]{1,0:T(8,128)}, f32[392,768]{1,0:T(8,128)}, f32[4,96,768]{2,1,0:T(8,128)}, f32[8,128]{1,0:T(8,128)}) custom-call(s32[1]{0:T(128)S(6)} %copy.19.live_ref, f32[392,768]{1,0:T(8,128)} %tokens_hbm.1, f32[392,768]{1,0:T(8,128)} %cotangent_hbm.1, bf16[3,96]{1,0:T(4,128)(2,1)} %gain_hbm.1, ...), custom_call_target="tpu_custom_call" | custom-call | tf_op jit(solution)/shard_map/layer/pallas_call | solution.py:1297
  181.0 3.9 %finish.1 = (f32[392,768]{1,0:T(8,128)}, f32[392,768]{1,0:T(8,128)}, f32[3,96]{1,0:T(4,128)}, f32[3,96,192]{2,1,0:T(8,128)}, f32[192,96]{1,0:T(8,128)}, /*index=...) custom-call(f32[392,768]{1,0:T(8,128)} %get-tuple-element.22.output_hbm, ...), custom_call_target="tpu_custom_call" | custom-call | tf_op jit(solution)/shard_map/finish/pallas_call | solution.py:1406

commit v3 on v2

--- a/solution.py
+++ b/solution.py
@@ -603,31 +603,31 @@
 BLOCK_ORDER = (1, 2, 3, 0)
 ORDER = (
     ("go",),
-    ("zs", 0, 2), ("line", 2, 0), ("line", 1, 0), ("zs", 0, 1), ("line", 0, 0), ("zs", 0, 3),
-    ("line", 0, 2), ("line", 0, 1), ("relay", 0, 0), ("zs", 1, 2), ("relay", 0, 2),
-    ("line", 0, 3), ("zs", 1, 3), ("line", 1, 2), ("zs", 1, 1), ("ln0",), ("across", 0, 0),
-    ("relay", 0, 3), ("relay", 0, 1), ("across", 0, 2), ("relay", 1, 0), ("zs", 2, 1),
-    ("zs", 2, 3), ("zs", 2, 2), ("mask",), ("relay", 1, 2), ("across", 0, 1), ("across", 0, 3),
-    ("line", 1, 3), ("zs", 3, 3), ("line", 1, 1), ("line", 2, 1), ("takeE0",), ("relay", 1, 3),
-    ("P0", 0), ("relay", 1, 1), ("P0", 1), ("line", 2, 3), ("P0", 2), ("P0", 3), ("line", 2, 2),
-    ("exch1",), ("relay", 2, 0), ("across", 1, 0), ("relay", 2, 1), ("relay", 2, 3),
-    ("line", 3, 0), ("zs", 3, 1), ("across", 1, 3), ("across", 1, 1), ("relay", 2, 2),
-    ("line", 3, 3), ("across", 1, 2), ("zs", 3, 2), ("ln1",), ("P1", 0), ("P1", 1),
-    ("line", 3, 1), ("P1", 2), ("across", 2, 3), ("across", 2, 0), ("across", 2, 1),
-    ("across", 2, 2), ("line", 3, 2), ("P1", 3), ("relay", 3, 0), ("ln2",), ("relay", 3, 3),
-    ("up", 0), ("relay", 3, 1), ("relay", 3, 2), ("up", 1), ("core", 0), ("across", 3, 3),
-    ("across", 3, 0), ("up", 2), ("core", 1), ("across", 3, 2), ("across", 3, 1), ("up", 3),
-    ("core", 2), ("first", 0), ("dn", 0), ("dn", 1), ("dn", 2), ("dn", 3), ("first", 1),
-    ("B1", 0), ("core", 3), ("B1", 1), ("second", 0), ("first", 2), ("core", 4), ("second", 1),
-    ("B1", 2), ("core", 5), ("B1", 3), ("nb2",), ("first", 4), ("second", 2), ("core", 6),
-    ("B2", 0), ("first", 5), ("core", 7), ("second", 4), ("B2", 1), ("core", 8), ("B2", 2),
-    ("first", 6), ("core", 9), ("second", 5), ("B2", 3), ("nb1",), ("core", 10), ("first", 9),
-    ("second", 6), ("first", 3), ("first", 10), ("first", 8), ("core", 11), ("first", 7),
-    ("second", 9), ("takeE2",), ("B3", 0), ("second", 10), ("B3", 1), ("second", 8), ("core", 12),
-    ("B3", 2), ("core", 13), ("B3", 3), ("first", 12), ("exch3",), ("second", 3), ("core", 14),
-    ("first", 13), ("second", 12), ("core", 15), ("first", 14), ("first", 11), ("second", 13),
-    ("third", 0), ("second", 7), ("nb0",), ("second", 14), ("first", 15), ("second", 11),
-    ("third", 2), ("third", 1), ("gain",), ("second", 15), ("third", 3),
+    ("line", 0, 0), ("zs", 0, 3), ("line", 2, 0), ("zs", 1, 1), ("zs", 0, 1), ("line", 1, 0),
+    ("zs", 0, 2), ("zs", 2, 1), ("line", 0, 3), ("zs", 1, 2), ("line", 1, 1), ("zs", 1, 3),
+    ("line", 0, 1), ("relay", 2, 0), ("ln0",), ("relay", 0, 3), ("line", 0, 2), ("across", 0, 3),
+    ("relay", 1, 1), ("across", 2, 0), ("zs", 2, 2), ("relay", 0, 0), ("relay", 0, 1),
+    ("relay", 0, 2), ("line", 2, 1), ("zs", 2, 3), ("line", 1, 2), ("mask",), ("zs", 3, 1),
+    ("line", 1, 3), ("across", 0, 0), ("across", 0, 1), ("across", 0, 2), ("zs", 3, 2),
+    ("takeE0",), ("P0", 0), ("across", 1, 1), ("line", 2, 2), ("relay", 1, 0), ("P0", 1),
+    ("P0", 2), ("relay", 1, 3), ("P0", 3), ("exch1",), ("relay", 1, 2), ("relay", 2, 2),
+    ("line", 2, 3), ("across", 1, 2), ("relay", 2, 1), ("across", 2, 2), ("line", 3, 2),
+    ("zs", 3, 3), ("across", 1, 0), ("across", 1, 3), ("relay", 2, 3), ("line", 3, 0),
+    ("line", 3, 1), ("ln1",), ("P1", 0), ("P1", 1), ("P1", 2), ("across", 2, 3), ("across", 2, 1),
+    ("line", 3, 3), ("relay", 3, 2), ("P1", 3), ("relay", 3, 0), ("ln2",), ("up", 0),
+    ("relay", 3, 1), ("relay", 3, 3), ("up", 1), ("across", 3, 0), ("across", 3, 2), ("core", 0),
+    ("up", 2), ("core", 1), ("across", 3, 1), ("across", 3, 3), ("up", 3), ("core", 2), ("dn", 0),
+    ("dn", 1), ("first", 0), ("dn", 2), ("dn", 3), ("first", 2), ("B1", 0), ("core", 3),
+    ("B1", 1), ("first", 1), ("second", 2), ("second", 0), ("core", 4), ("B1", 2), ("core", 5),
+    ("B1", 3), ("nb2",), ("second", 1), ("core", 6), ("B2", 0), ("core", 7), ("first", 5),
+    ("B2", 1), ("core", 8), ("B2", 2), ("core", 9), ("first", 6), ("second", 5), ("B2", 3),
+    ("nb1",), ("core", 10), ("first", 4), ("first", 8), ("second", 6), ("first", 10),
+    ("core", 11), ("first", 9), ("first", 7), ("second", 4), ("first", 3), ("takeE2",), ("B3", 0),
+    ("second", 10), ("B3", 1), ("core", 12), ("second", 8), ("B3", 2), ("second", 9),
+    ("core", 13), ("B3", 3), ("exch3",), ("core", 14), ("first", 13), ("second", 3), ("core", 15),
+    ("first", 14), ("first", 12), ("second", 13), ("first", 11), ("third", 0), ("second", 7),
+    ("first", 15), ("third", 1), ("second", 14), ("nb0",), ("second", 11), ("second", 12),
+    ("gain",), ("third", 2), ("second", 15), ("third", 3),
 )
 
 
@@ -642,7 +642,7 @@
 
 
 LINE_ACROSS = ()
-SUM_ACROSS = (0, 1)
+SUM_ACROSS = ()
 AFTER = after_each(ORDER)
 
 

time: 186 us -> 178 us (0.957)
  Pallas kernels: 184 us -> 177 us
    pallas_call x1, Pallas kernels: 180 us -> 173 us  [layer(): pl.pallas_call(layer_kernel, in_specs=[pl.BlockSpec(memory_space=pltpu.SM...]
where the time goes in v3:
time: 178 us
  Pallas kernels  177 us (99%)
    pallas_call x1, Pallas kernels, layer(): pl.pallas_call(layer_kernel, in_specs=[pl.BlockSpec(memory_space=pltpu.SM...  173 us
    pallas_call x1, Pallas kernels, finish(): pl.pallas_call(finish_kernel, in_specs=[there] * 3 + [pl.BlockSpec(memory...  3.88 us

profile of v3, /device:TPU:0, one launch (start us, length us, event | category | flops | bytes accessed | tf_op | source)
XLA Modules:
  0.0 178.3 jit_solution(15083635728800773623)
XLA Ops:
  1.3 172.9 %layer.1 = (bf16[4,4,768,768]{3,2,1,0:T(8,128)(2,1)}, f32[392,768]{1,0:T(8,128)}, f32[392,768]{1,0:T(8,128)}, f32[4,96,768]{2,1,0:T(8,128)}, f32[8,128]{1,0:T(8,128)}) custom-call(s32[1]{0:T(128)S(6)} %copy.19.live_ref, f32[392,768]{1,0:T(8,128)} %tokens_hbm.1, f32[392,768]{1,0:T(8,128)} %cotangent_hbm.1, bf16[3,96]{1,0:T(4,128)(2,1)} %gain_hbm.1, ...), custom_call_target="tpu_custom_call" | custom-call | tf_op jit(solution)/shard_map/layer/pallas_call | solution.py:1297
  174.2 3.9 %finish.1 = (f32[392,768]{1,0:T(8,128)}, f32[392,768]{1,0:T(8,128)}, f32[3,96]{1,0:T(4,128)}, f32[3,96,192]{2,1,0:T(8,128)}, f32[192,96]{1,0:T(8,128)}, /*index=...) custom-call(f32[392,768]{1,0:T(8,128)} %get-tuple-element.22.output_hbm, ...), custom_call_target="tpu_custom_call" | custom-call | tf_op jit(solution)/shard_map/finish/pallas_call | solution.py:1406

commit v4 on v3

--- a/solution.py
+++ b/solution.py
@@ -537,8 +537,9 @@
     heads = heads_ref.at[t]
     target = mixed_ref.at[t] if kind == "time" else sums
     units = attention_units(kind, count, width)
-    for batch in range(0, len(units), 6):
-        some = units[batch : batch + 6]
+    batch_size = 12 if kind == "time" else 6
+    for batch in range(0, len(units), batch_size):
+        some = units[batch : batch + batch_size]
         parts = [head_slices(heads, pl.ds(u[0], u[1]), width, u[5]) for u in some]
         scores = [
             mm(key, query * HEAD_DIM**-0.5, NT) + u[4] for u, (query, key, value) in zip(some, parts)

time: 178 us -> 178 us (level)
  no operation moved by 1% of the time
where the time goes in v4:
time: 178 us
  Pallas kernels  177 us (99%)
    pallas_call x1, Pallas kernels, layer(): pl.pallas_call(layer_kernel, in_specs=[pl.BlockSpec(memory_space=pltpu.SM...  173 us
    pallas_call x1, Pallas kernels, finish(): pl.pallas_call(finish_kernel, in_specs=[there] * 3 + [pl.BlockSpec(memory...  3.88 us

profile of v4, /device:TPU:0, one launch (start us, length us, event | category | flops | bytes accessed | tf_op | source)
XLA Modules:
  0.0 178.3 jit_solution(5923606956190457932)
XLA Ops:
  1.3 172.9 %layer.1 = (bf16[4,4,768,768]{3,2,1,0:T(8,128)(2,1)}, f32[392,768]{1,0:T(8,128)}, f32[392,768]{1,0:T(8,128)}, f32[4,96,768]{2,1,0:T(8,128)}, f32[8,128]{1,0:T(8,128)}) custom-call(s32[1]{0:T(128)S(6)} %copy.19.live_ref, f32[392,768]{1,0:T(8,128)} %tokens_hbm.1, f32[392,768]{1,0:T(8,128)} %cotangent_hbm.1, bf16[3,96]{1,0:T(4,128)(2,1)} %gain_hbm.1, ...), custom_call_target="tpu_custom_call" | custom-call | tf_op jit(solution)/shard_map/layer/pallas_call | solution.py:1298
  174.2 3.9 %finish.1 = (f32[392,768]{1,0:T(8,128)}, f32[392,768]{1,0:T(8,128)}, f32[3,96]{1,0:T(4,128)}, f32[3,96,192]{2,1,0:T(8,128)}, f32[192,96]{1,0:T(8,128)}, /*index=...) custom-call(f32[392,768]{1,0:T(8,128)} %get-tuple-element.22.output_hbm, ...), custom_call_target="tpu_custom_call" | custom-call | tf_op jit(solution)/shard_map/finish/pallas_call | solution.py:1407
